TPU v7x, 128 devices: a whole 4x4x4 slice. The times are simulated.
128 devices in a mesh: rows: 32 (over y, z, core), rhs: 4 (over x).
Axes of the slice: x: 4, y: 4, z: 4, core: 2. Of those that a mesh axis runs over, the one named last changes fastest.
Arguments:
- upper_unit: float32 [512, 128, 128], P('rows'), may hold values from -1 to 1, as said below
- lower_unit: float32 [512, 128, 128], P('rows'), may hold values from -1 to 1, as said below
- pivot_inv: float32 [512, 128, 128], P('rows'), may hold values from -0.25 to 2.25
- loss_grad_one: float32 [512, 128, 128], P('rows', 'rhs'), may hold values from -6 to 6
- loss_grad_two: float32 [512, 128, 128], P('rows', 'rhs'), may hold values from -0.046875 to 0.046875
- state_one: float32 [512, 128, 128], P('rows', 'rhs'), may hold values from -0.0029296875 to 0.0029296875
- state_two: float32 [512, 128, 128], P('rows', 'rhs'), may hold values from -1.5 to 1.5
Outputs:
- operator_grad: float32 [128, 3, 512, 128], P('rhs', None, 'rows')
Inputs may be any that keep to these rules, and one draw needn't show every extreme that they name: `upper_unit`: every block has spectral norm below 1. `lower_unit`: every block has spectral norm below 1.
All inputs are finite; a program needn't handle non-finite values.
Results may differ from a plain program's by a relative error of at most 0.0003.
Values sent between devices are 32-bit elements; how exact they have to be, the bound alone decides.
A program may use at most 128 MiB of HBM per device.

v0:
```python
import jax
import jax.numpy as jnp
from jax import lax
from jax.sharding import Mesh
from jax.sharding import PartitionSpec as P

ROWS = ("rows_0", "rows_1", "rows_2")


EXACT_ARITHMETIC = lax.Precision.HIGHEST


def with_halo(cells, sides, width):
    for axis, dim in sides:
        count = lax.axis_size(axis)
        ends = count - 1
        head = lax.slice_in_dim(cells, 0, width, axis=dim)
        tail = lax.slice_in_dim(cells, cells.shape[dim] - width, cells.shape[dim], axis=dim)
        cells = jnp.concatenate(
            [
                lax.ppermute(tail, axis, [(i, (i + 1) % count) for i in range(ends)]),
                cells,
                lax.ppermute(head, axis, [((i + 1) % count, i) for i in range(ends)]),
            ],
            axis=dim,
        )
    return cells


def copy_for_each(value, axis):
    size = lax.axis_size(axis)
    return lax.all_to_all(
        jnp.broadcast_to(value[None], (size, *value.shape)), axis, 0, 0, tiled=True
    )


def folded_in_pairs(pieces, combine):
    while len(jax.tree.leaves(pieces)[0]) > 1:
        pieces = jax.vmap(combine)(
            *(jax.tree.map(lambda part: part[side::2], pieces) for side in (0, 1))
        )
    return jax.tree.map(lambda part: part[0], pieces)


def prefix(value, axis, combine, identity):
    size, index = (lax.axis_size(axis), lax.axis_index(axis))
    passed = jnp.arange(size) < index

    def kept(part, zero, own):
        part = jnp.where(
            passed.reshape(-1, *(1 for _ in own.shape)), part, jnp.asarray(zero, own.dtype)
        )
        return part

    pieces = jax.tree.map(lambda part: copy_for_each(part, axis), value)
    return folded_in_pairs(jax.tree.map(kept, pieces, identity, value), combine)


def filled_with(value, identity):
    return jax.tree.map(
        lambda part, zero: jnp.zeros_like(part) + jnp.asarray(zero, part.dtype), value, identity
    )


def carried_in(value, axes, combine, identity):
    before = start = filled_with(value, identity)
    subtotal = value
    for axis in reversed(axes):
        size, index = (lax.axis_size(axis), lax.axis_index(axis))
        pieces = jax.tree.map(lambda part: lax.all_gather(part, axis), subtotal)
        inside, subtotal = (start, start)
        for k in reversed(range(size)):
            passed = k > index
            subtotal = combine(subtotal, jax.tree.map(lambda part: part[k], pieces))
            inside = jax.tree.map(lambda new, old: jnp.where(passed, new, old), subtotal, inside)
        before = combine(inside, before)
    return before


def chain_tables(factors, backward):
    length = factors.shape[0]
    tables = []
    current = factors
    offset = 1
    while offset < length:
        tables.append(current)
        if backward:
            joined = jnp.einsum(
                "jab,jbc->jac",
                current[offset:],
                current[: length - offset],
                precision=EXACT_ARITHMETIC,
            )
            current = jnp.concatenate([joined, current[length - offset :]], axis=0)
        else:
            joined = jnp.einsum(
                "jab,jbc->jac",
                current[: length - offset],
                current[offset:],
                precision=EXACT_ARITHMETIC,
            )
            current = jnp.concatenate([current[:offset], joined], axis=0)
        offset = offset * 2
    return (tables, current)


def chain_vectors(sources, tables, backward):
    length = sources.shape[0]
    current = sources
    offset = 1
    for level_mats in tables:
        if backward:
            shifted = jnp.einsum(
                "jrb,jbc->jrc",
                current[offset:],
                level_mats[: length - offset],
                precision=EXACT_ARITHMETIC,
            )
            current = jnp.concatenate(
                [shifted + current[: length - offset], current[length - offset :]], axis=0
            )
        else:
            shifted = jnp.einsum(
                "jrb,jbc->jrc",
                current[: length - offset],
                level_mats[offset:],
                precision=EXACT_ARITHMETIC,
            )
            current = jnp.concatenate([current[:offset], shifted + current[offset:]], axis=0)
        offset = offset * 2
    return current


def compose(former, latter):
    return (
        jnp.dot(former[0], latter[0], precision=EXACT_ARITHMETIC),
        jnp.dot(former[1], latter[0], precision=EXACT_ARITHMETIC) + latter[1],
    )


def block_grads(initial_rhs_group, later_rhs_group, padded):
    length = initial_rhs_group.shape[0]
    pieces = []
    for lead_row in (1, 0, 2):
        solution_past_opening = padded[0, lead_row : lead_row + length]
        solution_past_closing = padded[1, lead_row : lead_row + length]
        pieces.append(
            jnp.einsum(
                "ofz,ofl->zol", initial_rhs_group, solution_past_opening, precision=EXACT_ARITHMETIC
            )
            + jnp.einsum(
                "ofz,ofl->zol", later_rhs_group, solution_past_closing, precision=EXACT_ARITHMETIC
            )
        )
    return -jnp.stack(pieces, axis=1)


def body(upper_unit, lower_unit, pivot_inv, loss_grad_one, loss_grad_two, state_one, state_two):
    width = upper_unit.shape[1]
    upper_tables, upper_maps = chain_tables(-upper_unit, False)
    lower_tables, lower_maps = chain_tables(-lower_unit, True)
    upper_whole = upper_maps[-1]
    lower_whole = lower_maps[0]
    stacked = jnp.stack([state_one, state_two])
    padded = with_halo(stacked, ((ROWS, 1),), 1)
    identity = (jnp.eye(width, dtype=jnp.float32), jnp.zeros(loss_grad_one.shape[1:], jnp.float32))

    def solve(right_side):
        sources = jnp.einsum("jrb,jbc->jrc", right_side, upper_unit, precision=EXACT_ARITHMETIC)
        partial_value = chain_vectors(sources, upper_tables, False)
        incoming = prefix((upper_whole, partial_value[-1]), ROWS, compose, identity)[1]
        carried = (
            jnp.einsum("rb,jbc->jrc", incoming, upper_maps, precision=EXACT_ARITHMETIC)
            + partial_value
        )
        before = jnp.concatenate([incoming[None], carried[:-1]], axis=0)
        solved = jnp.einsum(
            "jrb,jbc->jrc", right_side - before, pivot_inv, precision=EXACT_ARITHMETIC
        )
        sources = jnp.einsum("jrb,jbc->jrc", solved, lower_unit, precision=EXACT_ARITHMETIC)
        partial_value = chain_vectors(sources, lower_tables, True)
        incoming = carried_in((lower_whole, partial_value[0]), ROWS, compose, identity)[1]
        carried = (
            jnp.einsum("rb,jbc->jrc", incoming, lower_maps, precision=EXACT_ARITHMETIC)
            + partial_value
        )
        following = jnp.concatenate([carried[1:], incoming[None]], axis=0)
        return solved - following

    adjoint_two = solve(loss_grad_two)
    adjoint_one = solve(loss_grad_one + adjoint_two)
    initial_rhs_group, later_rhs_group = (
        lax.all_to_all(adjoint_one, "rhs", split_axis=2, concat_axis=1, tiled=True),
        lax.all_to_all(adjoint_two, "rhs", split_axis=2, concat_axis=1, tiled=True),
    )
    collected_entries = lax.all_gather(padded, "rhs", axis=2, tiled=True)
    return block_grads(initial_rhs_group, later_rhs_group, collected_entries)


def solution(mesh):
    finer = Mesh(
        mesh.devices.reshape(4, 4, 2, mesh.shape["rhs"]), ("rows_0", "rows_1", "rows_2", "rhs")
    )
    in_specs = (
        P(ROWS, None, None),
        P(ROWS, None, None),
        P(ROWS, None, None),
        P(ROWS, "rhs", None),
        P(ROWS, "rhs", None),
        P(ROWS, "rhs", None),
        P(ROWS, "rhs", None),
    )
    out_specs = P("rhs", None, ROWS, None)
    return jax.shard_map(body, mesh=finer, in_specs=in_specs, out_specs=out_specs, check_vma=False)
```

profile of v0, /device:TPU:0, one launch (start us, length us, event | category | flops | bytes accessed | tf_op | source)
XLA Modules:
  0.0 253.4 jit_solution(11105732922872941929)
XLA Ops:
  6.5 1.4 neg.9
  17.3 8.4 %all-to-all-start = ((f32[32,32,128]{2,1,0:T(8,128)}), f32[32,32,128]{2,1,0:T(8,128)S(1)}, u32[]{:S(2)}, u32[]{:S(2)}) async-start(f32[32,32,128]{2,1,0:T(8,128)} %broadcast_in_dim.67), calls=%async_computation | async-start | bytes 1048576 | tf_op jit(solution)/shard_map/all_to_all | solution.py:32
  29.1 1.4 slice.655
  31.1 11.4 %all_gather.54 = f32[2,128,128]{2,1,0:T(8,128)S(1)} all-gather(f32[1,128,128]{2,1,0:T(8,128)S(1)} %slice.666), channel_id=1, replica_groups=mesh['rows_0'=4,'rows_1'=4,'rows_2'=2,'rhs'=4] {'rows_2'}, dimensions={0}, use_global_device_ids=true | all-gather | bytes 196608 | tf_op jit(solution)/shard_map/all_gather | solution.py:70
  43.7 12.9 %all-gather = f32[512,128]{1,0:T(8,128)S(1)} all-gather(f32[128,128]{1,0:T(8,128)S(1)} %fusion.130), channel_id=2, replica_groups=mesh['rows_0'=4,'rows_1'=4,'rows_2'=2,'rhs'=4] {'rows_1'}, dimensions={0}, use_global_device_ids=true | all-gather | bytes 327680 | tf_op jit(solution)/shard_map/all_gather | solution.py:70
  57.0 1.6 broadcast_in_dim.71
  58.5 6.9 %all-to-all-start.1 = ((f32[32,128,128]{2,1,0:T(8,128)}), f32[32,128,128]{2,1,0:T(8,128)}, u32[]{:S(2)}, u32[]{:S(2)}) async-start(f32[32,128,128]{2,1,0:T(8,128)} %broadcast_in_dim.71), calls=%async_computation.1 | async-start | bytes 4194304 | tf_op jit(solution)/shard_map/all_to_all | solution.py:32
  65.9 32.8 %all-gather.1 = f32[512,128]{1,0:T(8,128)S(1)} all-gather(f32[128,128]{1,0:T(8,128)S(1)} %fusion.132), channel_id=3, replica_groups=mesh['rows_0'=4,'rows_1'=4,'rows_2'=2,'rhs'=4] {'rows_0'}, dimensions={0}, use_global_device_ids=true | all-gather | bytes 327680 | tf_op jit(solution)/shard_map/all_gather | solution.py:70
  103.7 1.8 broadcast_select_fusion
  117.0 2.0 all_gather.59
  119.2 12.5 %all-gather.2 = f32[128,128]{1,0:T(8,128)S(1)} all-gather(f32[32,128]{1,0:T(8,128)S(1)} %convolution_add_fusion.42), channel_id=4, replica_groups=mesh['rows_0'=4,'rows_1'=4,'rows_2'=2,'rhs'=4] {'rows_1'}, dimensions={0}, use_global_device_ids=true | all-gather | bytes 81920 | tf_op jit(solution)/shard_map/all_gather | solution.py:70
  132.4 12.1 %all-gather.3 = f32[128,128]{1,0:T(8,128)S(1)} all-gather(f32[32,128]{1,0:T(8,128)S(1)} %convolution_add_fusion.39), channel_id=5, replica_groups=mesh['rows_0'=4,'rows_1'=4,'rows_2'=2,'rhs'=4] {'rows_0'}, dimensions={0}, use_global_device_ids=true | all-gather | bytes 81920 | tf_op jit(solution)/shard_map/all_gather | solution.py:70
  154.1 4.8 %all-to-all-start.2 = ((f32[32,32,128]{2,1,0:T(8,128)}), f32[32,32,128]{2,1,0:T(8,128)}, u32[]{:S(2)}, u32[]{:S(2)}) async-start(f32[32,32,128]{2,1,0:T(8,128)} %broadcast_in_dim.76), calls=%async_computation.2 | async-start | bytes 1048576 | tf_op jit(solution)/shard_map/all_to_all | solution.py:32
  159.7 2.1 collective-permute-start
  161.8 1.3 collective-permute-start.1
  163.2 2.9 %collective-permute-done.1 = f32[2,1,32,128]{3,2,1,0:T(8,128)S(1)} collective-permute-done((f32[2,1,32,128]{3,2,1,0:T(8,128)S(1)}, f32[2,1,32,128]{3,2,1,0:T(8,128)S(1)}, u32[]{:S(2)}, u32[]{:S(2)}) %collective-permute-start.1) | collective-permute-done | bytes 32800 | tf_op jit(solution)/shard_map/ppermute | solution.py:23
  166.1 1.9 pad_maximum_fusion.12
  168.0 2.3 copy.13
  170.3 2.4 reshape.83
  172.7 4.7 %all-to-all-start.4 = ((f32[4,1,16384]{2,1,0:T(1,128)}), f32[4,1,16384]{2,1,0:T(1,128)}, u32[]{:S(2)}, u32[]{:S(2)}) async-start(f32[4,1,16384]{2,1,0:T(1,128)} %reshape.83), calls=%async_computation.4 | async-start | bytes 524288 | tf_op jit(solution)/shard_map/all_to_all | solution.py:194
  177.5 1.3 broadcast_select_fusion.1
  187.4 4.3 %all_gather.64 = f32[2,32,128]{2,1,0:T(8,128)S(1)} all-gather(f32[1,32,128]{2,1,0:T(8,128)S(1)} %slice.711), channel_id=1, replica_groups=mesh['rows_0'=4,'rows_1'=4,'rows_2'=2,'rhs'=4] {'rows_2'}, dimensions={0}, use_global_device_ids=true | all-gather | bytes 49152 | tf_op jit(solution)/shard_map/all_gather | solution.py:70
  191.8 13.0 %all-gather.4 = f32[128,128]{1,0:T(8,128)S(1)} all-gather(f32[32,128]{1,0:T(8,128)S(1)} %convolution_add_fusion.34), channel_id=6, replica_groups=mesh['rows_0'=4,'rows_1'=4,'rows_2'=2,'rhs'=4] {'rows_1'}, dimensions={0}, use_global_device_ids=true | all-gather | bytes 81920 | tf_op jit(solution)/shard_map/all_gather | solution.py:70
  205.4 11.9 %all-gather.5 = f32[128,128]{1,0:T(8,128)S(1)} all-gather(f32[32,128]{1,0:T(8,128)S(1)} %convolution_add_fusion.31), channel_id=7, replica_groups=mesh['rows_0'=4,'rows_1'=4,'rows_2'=2,'rhs'=4] {'rows_0'}, dimensions={0}, use_global_device_ids=true | all-gather | bytes 81920 | tf_op jit(solution)/shard_map/all_gather | solution.py:70
  219.6 1.2 reshape.81
  220.8 4.8 %all-to-all-start.3 = ((f32[4,1,16384]{2,1,0:T(1,128)}), f32[4,1,16384]{2,1,0:T(1,128)}, u32[]{:S(2)}, u32[]{:S(2)}) async-start(f32[4,1,16384]{2,1,0:T(1,128)} %reshape.81), calls=%async_computation.3 | async-start | bytes 524288 | tf_op jit(solution)/shard_map/all_to_all | solution.py:193
  226.2 2.3 reduce.1
  230.1 2.3 all-to-all-done.3
  232.4 2.3 reduce
  236.3 2.4 fusion.19
  238.6 2.2 fusion.18
  245.0 1.3 copy.15
  (298 shorter events, 60.9 us)
Async XLA Ops:
  6.5 105.1 %copy-start = (f32[16,128,128]{2,1,0:T(8,128)S(1)}, f32[16,128,128]{2,1,0:T(8,128)}, u32[]{:S(2)}) copy-start(f32[16,128,128]{2,1,0:T(8,128)} %param.9) | copy-start | bytes 3145732
  15.6 10.2 %copy-start.4 = (f32[16,128,128]{2,1,0:T(8,128)S(1)}, f32[16,128,128]{2,1,0:T(8,128)}, u32[]{:S(2)}) copy-start(f32[16,128,128]{2,1,0:T(8,128)} %param.8) | copy-start | bytes 3145732
  16.4 10.5 %copy-start.51 = (f32[8,32,128]{2,1,0:T(8,128)}, f32[8,32,128]{2,1,0:T(8,128)S(1)}, u32[]{:S(2)}) copy-start(f32[8,32,128]{2,1,0:T(8,128)S(1)} %convolution_add_fusion.20) | copy-start | bytes 393220
  17.3 39.6 %all-to-all-start = ((f32[32,32,128]{2,1,0:T(8,128)}), f32[32,32,128]{2,1,0:T(8,128)S(1)}, u32[]{:S(2)}, u32[]{:S(2)}) async-start(f32[32,32,128]{2,1,0:T(8,128)} %broadcast_in_dim.67), calls=%async_computation | async-start | bytes 1048576 | tf_op jit(solution)/shard_map/all_to_all | solution.py:32
  29.0 13.9 %copy-start.33 = (f32[12,128,128]{2,1,0:T(8,128)}, f32[12,128,128]{2,1,0:T(8,128)S(1)}, u32[]{:S(2)}) copy-start(f32[12,128,128]{2,1,0:T(8,128)S(1)} %fusion.43) | copy-start | bytes 2359300
  29.0 13.9 %copy-start.37 = (f32[12,128,128]{2,1,0:T(8,128)S(1)}, f32[12,128,128]{2,1,0:T(8,128)}, u32[]{:S(2)}) copy-start(f32[12,128,128]{2,1,0:T(8,128)} %copy-done.36) | copy-start | bytes 2359300
  30.5 13.2 %copy-start.71 = (f32[4,128,128]{2,1,0:T(8,128)}, f32[4,128,128]{2,1,0:T(8,128)S(1)}, u32[]{:S(2)}) copy-start(f32[4,128,128]{2,1,0:T(8,128)S(1)} %slice.655) | copy-start | bytes 786436
  31.1 25.6 %copy-start.74 = (f32[8,128,128]{2,1,0:T(8,128)}, f32[8,128,128]{2,1,0:T(8,128)S(1)}, u32[]{:S(2)}) copy-start(f32[8,128,128]{2,1,0:T(8,128)S(1)} %fusion.9) | copy-start | bytes 1572868
  43.6 13.1 %copy-start.77 = (f32[8,128,128]{2,1,0:T(8,128)}, f32[8,128,128]{2,1,0:T(8,128)S(1)}, u32[]{:S(2)}) copy-start(f32[8,128,128]{2,1,0:T(8,128)S(1)} %fusion.11) | copy-start | bytes 1572868
  58.5 45.2 %all-to-all-start.1 = ((f32[32,128,128]{2,1,0:T(8,128)}), f32[32,128,128]{2,1,0:T(8,128)}, u32[]{:S(2)}, u32[]{:S(2)}) async-start(f32[32,128,128]{2,1,0:T(8,128)} %broadcast_in_dim.71), calls=%async_computation.1 | async-start | bytes 4194304 | tf_op jit(solution)/shard_map/all_to_all | solution.py:32
  98.7 5.0 %copy-start.80 = (pred[32]{0:T(512)(128)(4,1)}, pred[32]{0:T(512)(128)(4,1)S(1)}, u32[]{:S(2)}) copy-start(pred[32]{0:T(512)(128)(4,1)S(1)} %iota_compare_fusion.12) | copy-start | bytes 100
  114.6 17.1 %copy-start.65 = (f32[32,128]{1,0:T(8,128)S(1)}, f32[32,128]{1,0:T(8,128)}, u32[]{:S(2)}) copy-start(f32[32,128]{1,0:T(8,128)} %fusion.126) | copy-start | bytes 49156
  115.5 16.7 %copy-start.49 = (f32[128,128]{1,0:T(8,128)S(1)}, f32[128,128]{1,0:T(8,128)}, u32[]{:S(2)}) copy-start(f32[128,128]{1,0:T(8,128)} %copy-done.48) | copy-start | bytes 196612
  115.6 29.0 %copy-start.30 = (f32[512,128]{1,0:T(8,128)S(1)}, f32[512,128]{1,0:T(8,128)}, u32[]{:S(2)}) copy-start(f32[512,128]{1,0:T(8,128)} %copy-done.29) | copy-start | bytes 786436
  115.6 28.9 %copy-start.63 = (f32[32,128]{1,0:T(8,128)S(1)}, f32[32,128]{1,0:T(8,128)}, u32[]{:S(2)}) copy-start(f32[32,128]{1,0:T(8,128)} %fusion.103) | copy-start | bytes 49156
  115.6 29.5 %copy-start.61 = (f32[128,128]{1,0:T(8,128)S(1)}, f32[128,128]{1,0:T(8,128)}, u32[]{:S(2)}) copy-start(f32[128,128]{1,0:T(8,128)} %fusion.109) | copy-start | bytes 196612
  115.6 29.8 %copy-start.69 = (f32[4,128,128]{2,1,0:T(8,128)S(1)}, f32[4,128,128]{2,1,0:T(8,128)}, u32[]{:S(2)}) copy-start(f32[4,128,128]{2,1,0:T(8,128)} %copy-done.68) | copy-start | bytes 786436
  115.6 29.8 %copy-start.75 = (f32[8,128,128]{2,1,0:T(8,128)S(1)}, f32[8,128,128]{2,1,0:T(8,128)}, u32[]{:S(2)}) copy-start(f32[8,128,128]{2,1,0:T(8,128)} %copy-done.74) | copy-start | bytes 1572868
  117.0 29.1 %copy-start.67 = (f32[16,32,128]{2,1,0:T(8,128)S(1)}, f32[16,32,128]{2,1,0:T(8,128)}, u32[]{:S(2)}) copy-start(f32[16,32,128]{2,1,0:T(8,128)} %param.10) | copy-start | bytes 786436
  154.1 18.6 %all-to-all-start.2 = ((f32[32,32,128]{2,1,0:T(8,128)}), f32[32,32,128]{2,1,0:T(8,128)}, u32[]{:S(2)}, u32[]{:S(2)}) async-start(f32[32,32,128]{2,1,0:T(8,128)} %broadcast_in_dim.76), calls=%async_computation.2 | async-start | bytes 1048576 | tf_op jit(solution)/shard_map/all_to_all | solution.py:32
  158.9 77.3 %all-gather.8.cloned.1.call-start = ((), (), s32[]{:S(2)}) async-start(), calls=%async_computation.5 | async-start | bytes 2949120 | tf_op jit(solution)/shard_map/all_gather | solution.py:196
  159.7 3.4 %collective-permute-start = (f32[2,1,32,128]{3,2,1,0:T(8,128)S(1)}, f32[2,1,32,128]{3,2,1,0:T(8,128)S(1)}, u32[]{:S(2)}, u32[]{:S(2)}) collective-permute-start(f32[2,1,32,128]{3,2,1,0:T(8,128)S(1)} %get-tuple-element.7), channel_id=1, source_target_pairs={{0,4},{4,8},{8,12},{12,16},{16,20},{20,24},{24,28},{28,32},{32,36}... | collective-permute-start | bytes 98312 | tf_op jit(solution)/shard_map/ppermute | solution.py:21
  161.8 4.2 %collective-permute-start.1 = (f32[2,1,32,128]{3,2,1,0:T(8,128)S(1)}, f32[2,1,32,128]{3,2,1,0:T(8,128)S(1)}, u32[]{:S(2)}, u32[]{:S(2)}) collective-permute-start(f32[2,1,32,128]{3,2,1,0:T(8,128)S(1)} %get-tuple-element.8), channel_id=1, source_target_pairs={{4,0},{8,4},{12,8},{16,12},{20,16},{24,20},{28,24},{32,28},{36,32}... | collective-permute-start | bytes 98312 | tf_op jit(solution)/shard_map/ppermute | solution.py:23
  172.7 48.1 %all-to-all-start.4 = ((f32[4,1,16384]{2,1,0:T(1,128)}), f32[4,1,16384]{2,1,0:T(1,128)}, u32[]{:S(2)}, u32[]{:S(2)}) async-start(f32[4,1,16384]{2,1,0:T(1,128)} %reshape.83), calls=%async_computation.4 | async-start | bytes 524288 | tf_op jit(solution)/shard_map/all_to_all | solution.py:194
  185.0 19.9 %copy-start.66 = (f32[32,128]{1,0:T(8,128)S(1)}, f32[32,128]{1,0:T(8,128)}, u32[]{:S(2)}) copy-start(f32[32,128]{1,0:T(8,128)} %fusion.126) | copy-start | bytes 49156
  185.9 31.4 %copy-start.31 = (f32[512,128]{1,0:T(8,128)S(1)}, f32[512,128]{1,0:T(8,128)}, u32[]{:S(2)}) copy-start(f32[512,128]{1,0:T(8,128)} %copy-done.29) | copy-start | bytes 786436
  185.9 31.4 %copy-start.64 = (f32[32,128]{1,0:T(8,128)S(1)}, f32[32,128]{1,0:T(8,128)}, u32[]{:S(2)}) copy-start(f32[32,128]{1,0:T(8,128)} %fusion.103) | copy-start | bytes 49156
  185.9 31.9 %copy-start.62 = (f32[128,128]{1,0:T(8,128)S(1)}, f32[128,128]{1,0:T(8,128)}, u32[]{:S(2)}) copy-start(f32[128,128]{1,0:T(8,128)} %fusion.109) | copy-start | bytes 196612
  185.9 32.1 %copy-start.50 = (f32[128,128]{1,0:T(8,128)S(1)}, f32[128,128]{1,0:T(8,128)}, u32[]{:S(2)}) copy-start(f32[128,128]{1,0:T(8,128)} %copy-done.48) | copy-start | bytes 196612
  185.9 32.4 %copy-start.70 = (f32[4,128,128]{2,1,0:T(8,128)S(1)}, f32[4,128,128]{2,1,0:T(8,128)}, u32[]{:S(2)}) copy-start(f32[4,128,128]{2,1,0:T(8,128)} %copy-done.68) | copy-start | bytes 786436
  186.0 32.4 %copy-start.76 = (f32[8,128,128]{2,1,0:T(8,128)S(1)}, f32[8,128,128]{2,1,0:T(8,128)}, u32[]{:S(2)}) copy-start(f32[8,128,128]{2,1,0:T(8,128)} %copy-done.74) | copy-start | bytes 1572868
  220.8 11.6 %all-to-all-start.3 = ((f32[4,1,16384]{2,1,0:T(1,128)}), f32[4,1,16384]{2,1,0:T(1,128)}, u32[]{:S(2)}, u32[]{:S(2)}) async-start(f32[4,1,16384]{2,1,0:T(1,128)} %reshape.81), calls=%async_computation.3 | async-start | bytes 524288 | tf_op jit(solution)/shard_map/all_to_all | solution.py:193
  (57 other events, 127.6 us)
Sparse Core Ops, SparseCore 0:
  168.1 37.8 all-gather.7
where the time goes:
time: 258 us; the launch traced here: 253 us
  blocking collectives  113 us (44%)
  matrix products  51.6 us (20%)
  starting transfers between devices  33.1 us (13%)
  local copies, waits for them, and re-layouts  20.2 us (8%)
  between operations  15.5 us (6%)
  other arithmetic  14.8 us (6%)
  waiting for transfers between devices  5.32 us (2%)
    all_gather x9, blocking collectives, carried_in(): pieces = jax.tree.map(lambda part: lax.all_gather(part, axis), subtotal)  113 us
    all_to_all x3, starting transfers between devices, copy_for_each(): lax.all_to_all(jnp.broadcast_to(value[None], (size, *value.shape)), axis,...  20.1 us
    dot_general x33, matrix products, compose(): jnp.dot(former[1], latter[0], precision=EXACT_ARITHMETIC) + latter[1]  9.45 us
    unnamed x166, local copies, waits for them, and re-layouts  8.46 us
    dot_general x8, matrix products, chain_vectors(): jnp.einsum('jrb,jbc->jrc', current[:length - offset], level_mats[offset:]...  6.4 us
    dot_general x8, matrix products, chain_vectors(): jnp.einsum('jrb,jbc->jrc', current[offset:], level_mats[:length - offset]...  6.39 us
    dot_general x3, matrix products, block_grads(): jnp.einsum('ofz,ofl->zol', initial_rhs_group, solution_past_opening, prec...  5.62 us
  transfers between devices with their start and end apart: 8, of which 2 were waited for; matrix products, arithmetic and copies ran while one was open for 16% of the time, Pallas kernels for 0%

commit v1 on v0

v1 whole, which is shorter than its diff:
```python
import jax
import jax.numpy as jnp
from jax import lax
from jax.experimental import pallas as pl
from jax.experimental.pallas import tpu as pltpu
from jax.sharding import PartitionSpec as P

MESH = pl.DeviceIdType.MESH
F32, BF16 = jnp.float32, jnp.bfloat16
N = 16
W = 128
R = 32
EM, EN, EK, EF, EH, ES = 0, 128, 256, 384, 416, 448


def split(x):
    hi = x.astype(BF16)
    lo = (x - hi.astype(F32)).astype(BF16)
    return hi, lo


def tile_of(w):
    hi, lo = split(w)
    row = jnp.concatenate([hi, lo], axis=1)
    return jnp.concatenate([row, row], axis=0)


def mm(x, tile):
    hi, lo = split(x)
    both = jnp.concatenate([hi, lo], axis=1)
    out = jnp.dot(both, tile, preferred_element_type=F32)
    return out[:, :W] + out[:, W:]


def mm_pair(a, l, tile):
    ah, al = split(a)
    lh, ll = split(l)
    hi = jnp.concatenate([ah, lh], axis=1)
    lo = jnp.concatenate([al, ll], axis=1)
    out = jnp.dot(jnp.concatenate([hi, lo], axis=0), tile, preferred_element_type=F32)
    m = a.shape[0]
    out = out[:m] + out[m:]
    return out[:, :W] + out[:, W:]


def kernel(
    u_ref, l_ref, p_ref, g1_ref, g2_ref, s1_ref, s2_ref, out_ref,
    tu, tp, tl, tab, zs, v2, v1,
    g_c, g_z, g_y, t_c, t_z, t_y, h_c, h_z, h_y, r_c, r_z, ae, le,
    sg, halo, ss, ps, pr, lt,
    sem_c, sem_z, sem_y, sem_hc, sem_hz, sem_hy, sem_s, sem_own, sem_halo, sem_p,
):
    d = lax.axis_index("rows")
    x = lax.axis_index("rhs")
    y, z, c = d // 8, (d // 2) % 4, d % 2

    def in_c(j):
        return (y * 8 + z * 2 + (c + j) % 2, x)

    def in_z(j):
        return (y * 8 + ((z + j) % 4) * 2 + c, x)

    def in_y(j):
        return (((y + j) % 4) * 8 + z * 2 + c, x)

    def in_x(j):
        return (d, (x + j) % 4)

    after, before = ((d + 1) % 32, x), ((d + 31) % 32, x)

    barrier = pltpu.get_barrier_semaphore()
    peers = [in_c(1)] + [f(j) for f in (in_z, in_y, in_x) for j in (1, 2, 3)] + [after, before]
    for peer in peers:
        pl.semaphore_signal(barrier, inc=1, device_id=peer, device_id_type=MESH)
    pl.semaphore_wait(barrier, len(peers))

    own = [
        pltpu.make_async_copy(s, sg.at[x, t], sem_own.at[t]) for t, s in enumerate((s1_ref, s2_ref))
    ]
    for copy in own:
        copy.start()
    for copy in own:
        copy.wait()
    states = [
        pltpu.make_async_remote_copy(
            src_ref=sg.at[x], dst_ref=sg.at[x],
            send_sem=sem_s.at[0, j - 1], recv_sem=sem_s.at[1, j - 1],
            device_id=in_x(j), device_id_type=MESH,
        )
        for j in (1, 3, 2)
    ]
    for copy in states:
        copy.start()

    def spread(ref, me, size, where, sem):
        copies = [
            pltpu.make_async_remote_copy(
                src_ref=ref.at[me], dst_ref=ref.at[me],
                send_sem=sem.at[0, j - 1], recv_sem=sem.at[1, j - 1],
                device_id=where(j), device_id_type=MESH,
            )
            for j in range(1, size)
        ]
        for copy in copies:
            copy.start()
        return copies

    def finish(copies):
        for copy in copies:
            copy.wait()

    eye = (
        lax.broadcasted_iota(jnp.int32, (W, W), 0) == lax.broadcasted_iota(jnp.int32, (W, W), 1)
    ).astype(F32)
    zero_m = jnp.zeros((W, W), F32)
    zero_v = jnp.zeros((R, W), F32)

    def up_first(i, carry):
        tile = tile_of(u_ref[i])
        tu[i] = tile
        tile_p = tile_of(p_ref[i])
        tp[i] = tile_p
        yv = jnp.concatenate([g2_ref[i], zero_m], axis=0) - carry
        zs[i] = mm(yv, tile_p)
        return mm(yv, tile)

    carry = lax.fori_loop(0, N, up_first, jnp.concatenate([zero_v, eye], axis=0))
    g_c[c, EF:EH] = carry[:R]
    g_c[c, EM:EN] = carry[R:]

    def down_first(k, carry):
        i = N - 1 - k
        tile = tile_of(l_ref[i])
        tl[i] = tile
        vv = jnp.concatenate([zs[i], zero_m], axis=0) - carry
        v2[i] = vv[:R]
        hi, lo = split(vv[R:])
        tab[i] = jnp.concatenate([hi, lo], axis=1)
        return mm(vv, tile)

    carry = lax.fori_loop(0, N, down_first, jnp.concatenate([zero_v, zero_m, eye], axis=0))
    g_c[c, EH:ES] = carry[:R]
    g_c[c, EN:EK] = carry[R : R + W]
    g_c[c, EK:EF] = carry[R + W :]

    def gather_first(g, t, me, size, where, sem):
        copies = spread(g, me, size, where, sem)
        finish(copies)
        for e in range(size):
            for m in range(3):
                t[e, m] = tile_of(g[e, m * W : (m + 1) * W])

    def level_maps(g, t, r, me, size):
        a = jnp.concatenate([zero_v, eye], axis=0)
        many = []
        for e in range(size):
            ae[e] = a
            many.append(a)
            a = mm(a, t[e, 0]) + jnp.concatenate([g[e, EF:EH], zero_m], axis=0)
        l = jnp.concatenate([zero_v, zero_m, eye], axis=0)
        for e in reversed(range(size)):
            le[e] = l
            source = jnp.concatenate([g[e, EH:ES], zero_m], axis=0) + mm(many[e], t[e, 1])
            l = mm(l, t[e, 2]) + jnp.concatenate([source, zero_m], axis=0)
        r[0] = tile_of(ae[me, R:])
        r[1] = tile_of(le[me, R : R + W])
        r[2] = tile_of(le[me, R + W :])
        return (a, l), (ae[me, :R], le[me, :R])

    def level(vec, t, me, size):
        a = zero_v
        many = []
        for e in range(size):
            ae[e, :R] = a
            many.append(a)
            a = mm(a, t[e, 0]) + vec(e, 0)
        l = zero_v
        for e in reversed(range(size)):
            le[e, :R] = l
            l = mm(l, t[e, 2]) + (vec(e, 1) + mm(many[e], t[e, 1]))
        return (a, l), (ae[me, :R], le[me, :R])

    def put(g, me, a, l):
        g[me, EF:EH] = a[:R]
        g[me, EM:EN] = a[R:]
        g[me, EH:ES] = l[:R]
        g[me, EN:EK] = l[R : R + W]
        g[me, EK:EF] = l[R + W :]

    def enter(inside, r, a, l):
        return inside[0] + mm(a, r[0]), inside[1] + mm(a, r[1]) + mm(l, r[2])

    def vec_of(g):
        return lambda e, side: g[e, EF + R * side : EF + R * side + R]

    def vec_small(h):
        return lambda e, side: h[e, R * side : R * side + R]

    gather_first(g_c, t_c, c, 2, in_c, sem_c)
    total, inside_c = level_maps(g_c, t_c, r_c, c, 2)
    put(g_z, z, *total)
    gather_first(g_z, t_z, z, 4, in_z, sem_z)
    total, inside_z = level_maps(g_z, t_z, r_z, z, 4)
    put(g_y, y, *total)
    gather_first(g_y, t_y, y, 4, in_y, sem_y)
    _, (a, l) = level(vec_of(g_y), t_y, y, 4)
    a, l = enter(inside_z, r_z, a, l)
    a, l = enter(inside_c, r_c, a, l)

    def settle(v, a, l):
        def one(i, none):
            v[i] = v[i] + mm_pair(a, l, tab[i])
            return none

        lax.fori_loop(0, N, one, 0)

    settle(v2, a, l)

    block_of = lax.broadcasted_iota(jnp.int32, (W, W), 1) // R

    def share(v, t):
        groups = [v[4 * q : 4 * q + 4].reshape(W, W) for q in range(4)]
        for dest in range(4):
            piece = groups[dest]
            for q in range(4):
                if q != dest:
                    moved = pltpu.roll(groups[q], (R * (q - dest)) % W, 1)
                    piece = jnp.where(block_of == q, moved, piece)
            if True:
                own_q = groups[dest]
                piece = jnp.where(block_of == dest, own_q, piece)
            ps[t, dest] = piece
        pr[t, x] = ps[t, x]
        copies = [
            pltpu.make_async_remote_copy(
                src_ref=ps.at[t, (x + j) % 4], dst_ref=pr.at[t, x],
                send_sem=sem_p.at[t, 0, j - 1], recv_sem=sem_p.at[t, 1, j - 1],
                device_id=in_x(j), device_id_type=MESH,
            )
            for j in (1, 3, 2)
        ]
        for copy in copies:
            copy.start()
        return copies

    shared_two = share(v2, 1)

    def up(i, carry):
        yv = g1_ref[i] + v2[i] - carry
        zs[i, :R] = mm(yv, tp[i])
        return mm(yv, tu[i])

    h_c[c, :R] = lax.fori_loop(0, N, up, zero_v)

    def down(k, carry):
        i = N - 1 - k
        vv = zs[i, :R] - carry
        v1[i] = vv
        return mm(vv, tl[i])

    h_c[c, R:] = lax.fori_loop(0, N, down, zero_v)

    finish(spread(h_c, c, 2, in_c, sem_hc))
    (a, l), inside_c = level(vec_small(h_c), t_c, c, 2)
    h_z[z, :R] = a
    h_z[z, R:] = l
    in_flight = spread(h_z, z, 4, in_z, sem_hz)

    finish(states)
    edges = []
    for side, (row, where) in enumerate(((N - 1, after), (0, before))):
        for q in range(4):
            copy = pltpu.make_async_remote_copy(
                src_ref=sg.at[q, :, row], dst_ref=halo.at[side, q],
                send_sem=sem_halo.at[0, side, q], recv_sem=sem_halo.at[1, side, q],
                device_id=where, device_id_type=MESH,
            )
            copy.start()
            edges.append(copy)

    def operand(parts):
        hi, lo = split(jnp.concatenate(parts, axis=0))
        return jnp.concatenate([hi, lo], axis=1)

    def pack(i, none):
        ss[i + 1] = operand([sg[q, t, i] for t in range(2) for q in range(4)])
        return none

    lax.fori_loop(0, N, pack, 0)

    finish(in_flight)
    (a, l), inside_z = level(vec_small(h_z), t_z, z, 4)
    h_y[y, :R] = a
    h_y[y, R:] = l
    in_flight = spread(h_y, y, 4, in_y, sem_hy)

    finish(edges)
    keep = ((d > 0).astype(F32), (d < 31).astype(F32))
    for side, slot in ((0, 0), (1, N + 1)):
        ss[slot] = operand([halo[side, q, t] * keep[side] for t in range(2) for q in range(4)])

    finish(in_flight)
    _, (a, l) = level(vec_small(h_y), t_y, y, 4)
    a, l = enter(inside_z, r_z, a, l)
    a, l = enter(inside_c, r_c, a, l)
    settle(v1, a, l)
    finish(shared_two)
    shared_one = share(v1, 0)

    def turn(t):
        for sub in range(4):
            stack = jnp.concatenate(
                [pr[t, q, R * sub : R * sub + R] for q in range(4)], axis=0
            ).T
            hi, lo = split(stack)
            for q in range(4):
                lt[4 * q + sub, :R, t * W : (t + 1) * W] = hi[R * q : R * q + R]
                lt[4 * q + sub, R:, t * W : (t + 1) * W] = lo[R * q : R * q + R]

    turn(1)
    finish(shared_one)
    turn(0)

    def grads(i, none):
        for k, j in enumerate((1, 0, 2)):
            o = jnp.dot(lt[i], ss[i + j], preferred_element_type=F32)
            o = o[:R] + o[R:]
            out_ref[k, i] = -(o[:, :W] + o[:, W:])
        return none

    lax.fori_loop(0, N, grads, 0)


def body(upper_unit, lower_unit, pivot_inv, loss_grad_one, loss_grad_two, state_one, state_two):
    vmem = pl.BlockSpec(memory_space=pltpu.VMEM)
    anywhere = pl.BlockSpec(memory_space=pl.ANY)
    dma = pltpu.SemaphoreType.DMA
    tile = (2 * W, 2 * W)
    grads = pl.pallas_call(
        kernel,
        out_shape=jax.ShapeDtypeStruct((3, N, R, W), F32),
        in_specs=[vmem] * 5 + [anywhere] * 2,
        out_specs=vmem,
        scratch_shapes=[
            pltpu.VMEM((N, *tile), BF16),
            pltpu.VMEM((N, *tile), BF16),
            pltpu.VMEM((N, *tile), BF16),
            pltpu.VMEM((N, *tile), BF16),
            pltpu.VMEM((N, R + W, W), F32),
            pltpu.VMEM((N, R, W), F32),
            pltpu.VMEM((N, R, W), F32),
            pltpu.VMEM((2, ES, W), F32),
            pltpu.VMEM((4, ES, W), F32),
            pltpu.VMEM((4, ES, W), F32),
            pltpu.VMEM((2, 3, *tile), BF16),
            pltpu.VMEM((4, 3, *tile), BF16),
            pltpu.VMEM((4, 3, *tile), BF16),
            pltpu.VMEM((2, 2 * R, W), F32),
            pltpu.VMEM((4, 2 * R, W), F32),
            pltpu.VMEM((4, 2 * R, W), F32),
            pltpu.VMEM((3, *tile), BF16),
            pltpu.VMEM((3, *tile), BF16),
            pltpu.VMEM((4, R + W, W), F32),
            pltpu.VMEM((4, R + 2 * W, W), F32),
            pltpu.VMEM((4, 2, N, R, W), F32),
            pltpu.VMEM((2, 4, 2, R, W), F32),
            pltpu.VMEM((N + 2, *tile), BF16),
            pltpu.VMEM((2, 4, W, W), F32),
            pltpu.VMEM((2, 4, W, W), F32),
            pltpu.VMEM((N, 2 * R, 2 * W), BF16),
            dma((2, 1)), dma((2, 3)), dma((2, 3)),
            dma((2, 1)), dma((2, 3)), dma((2, 3)),
            dma((2, 3)), dma((2,)), dma((2, 2, 4)), dma((2, 2, 3)),
        ],
        compiler_params=pltpu.CompilerParams(
            collective_id=0, has_side_effects=True, vmem_limit_bytes=60 * 2**20
        ),
    )(upper_unit, lower_unit, pivot_inv, loss_grad_one, loss_grad_two, state_one, state_two)
    return jnp.transpose(grads, (2, 0, 1, 3))


def solution(mesh):
    by_rows = P("rows", None, None)
    by_both = P("rows", "rhs", None)
    return jax.shard_map(
        body,
        mesh=mesh,
        in_specs=(by_rows,) * 3 + (by_both,) * 4,
        out_specs=P("rhs", None, "rows", None),
        check_vma=False,
    )
```

time: 258 us -> 80.5 us (0.31); the launches traced: 253 us -> 80.3 us
  blocking collectives: 113 us -> 0 us
  Pallas kernels: 0 us -> 77.8 us
  matrix products: 51.6 us -> 0 us
  starting transfers between devices: 33.1 us -> 0 us
  local copies, waits for them, and re-layouts: 20.2 us -> 2.47 us
  between operations: 15.5 us -> 0.01 us
  other arithmetic: 14.8 us -> 0 us
  waiting for transfers between devices: 5.32 us -> 0 us
    all_gather x9 -> x0, blocking collectives: 113 us -> none  [carried_in(): pieces = jax.tree.map(lambda part: lax.all_gather(part, axis), subtotal)]
    pallas_call x0 -> x1, Pallas kernels: none -> 77.8 us  [body(): pl.pallas_call(kernel, out_shape=jax.ShapeDtypeStruct((3, N, R, W), F32),...]
    dot_general x84 -> x0, matrix products: 51.4 us -> none  [the longest x33 9.45 us: compose(): jnp.dot(former[1], latter[0], precision=EXACT_ARITHMETIC) + latter[1]]
    all_to_all x5 -> x0, starting transfers between devices: 29.6 us -> none  [the longest x3 20.1 us: copy_for_each(): lax.all_to_all(jnp.broadcast_to(value[None], (size, *value.shape)), axis,...]
    unnamed x166 -> x0, local copies, waits for them, and re-layouts: 8.46 us -> none
    all_to_all x2 -> x0, other arithmetic: 4.62 us -> none  [the longest x1 2.31 us: body(): lax.all_to_all(adjoint_one, 'rhs', split_axis=2, concat_axis=1, tiled=True)]
    select_n x3 -> x0, other arithmetic: 4.03 us -> none  [kept(): jnp.where(passed.reshape(-1, *(1 for _ in own.shape)), part, jnp.asarray(...]
    ppermute x2 -> x0, starting transfers between devices: 3.39 us -> none  [the longest x1 2.09 us: with_halo(): lax.ppermute(tail, axis, [(i, (i + 1) % count) for i in range(ends)])]
  transfers between devices with their start and end apart: 8 -> 0, of which waited for: 2 -> 0; matrix products, arithmetic and copies ran while one was open for 16% -> 0% of each run, Pallas kernels for 0% -> 0%
where the time goes in v1:
time: 80.5 us; the launch traced here: 80.3 us
  Pallas kernels  77.8 us (97%)
  local copies, waits for them, and re-layouts  2.47 us (3%)
    pallas_call x1, Pallas kernels, body(): pl.pallas_call(kernel, out_shape=jax.ShapeDtypeStruct((3, N, R, W), F32),...  77.8 us
    transpose x1, local copies, waits for them, and re-layouts, body(): return jnp.transpose(grads, (2, 0, 1, 3))  2.47 us

profile of v1, /device:TPU:0, one launch (start us, length us, event | category | flops | bytes accessed | tf_op | source)
XLA Modules:
  0.0 80.3 jit_solution(46147670358291148)
XLA Ops:
  0.0 77.8 %shard_map.73 = f32[3,16,32,128]{3,2,1,0:T(8,128)} custom-call(f32[16,128,128]{2,1,0:T(8,128)} %u_ref.1, f32[16,128,128]{2,1,0:T(8,128)} %l_ref.1, f32[16,128,128]{2,1,0:T(8,128)} %p_ref.1, f32[16,32,128]{2,1,0:T(8,128)} %g1_ref.1, f32[16,32,128]{2,1,0:T(8,128)} %g2_ref.1, f32[16,32,128]{2,1,0:T(8,128)} %s1_ref.1, f32[16,32,128]{2,1,0:T(8,128)} %s2_ref.1), custom_call_target="tpu_custom_call" | custom-call | tf_op jit(solution)/shard_map/pallas_call | solution.py:339
  77.8 2.5 %copy.8 = f32[32,3,16,128]{3,2,1,0:T(8,128)} copy(f32[32,3,16,128]{3,0,2,1:T(8,128)} %bitcast.1) | data formatting | bytes 1572864 | tf_op jit(solution)/shard_map/transpose | solution.py:379

commit v2 on v1

--- a/solution.py
+++ b/solution.py
@@ -72,15 +72,12 @@
     peers = [in_c(1)] + [f(j) for f in (in_z, in_y, in_x) for j in (1, 2, 3)] + [after, before]
     for peer in peers:
         pl.semaphore_signal(barrier, inc=1, device_id=peer, device_id_type=MESH)
-    pl.semaphore_wait(barrier, len(peers))
 
     own = [
         pltpu.make_async_copy(s, sg.at[x, t], sem_own.at[t]) for t, s in enumerate((s1_ref, s2_ref))
     ]
     for copy in own:
         copy.start()
-    for copy in own:
-        copy.wait()
     states = [
         pltpu.make_async_remote_copy(
             src_ref=sg.at[x], dst_ref=sg.at[x],
@@ -89,8 +86,14 @@
         )
         for j in (1, 3, 2)
     ]
-    for copy in states:
-        copy.start()
+
+    def run(steps, step, carry, by=4):
+        def some(b, carry):
+            for s in range(by):
+                carry = step(b * by + s, carry)
+            return carry
+
+        return lax.fori_loop(0, steps // by, some, carry)
 
     def spread(ref, me, size, where, sem):
         copies = [
@@ -124,7 +127,12 @@
         zs[i] = mm(yv, tile_p)
         return mm(yv, tile)
 
-    carry = lax.fori_loop(0, N, up_first, jnp.concatenate([zero_v, eye], axis=0))
+    carry = run(N, up_first, jnp.concatenate([zero_v, eye], axis=0))
+    pl.semaphore_wait(barrier, len(peers))
+    for copy in own:
+        copy.wait()
+    for copy in states:
+        copy.start()
     g_c[c, EF:EH] = carry[:R]
     g_c[c, EM:EN] = carry[R:]
 
@@ -138,14 +146,38 @@
         tab[i] = jnp.concatenate([hi, lo], axis=1)
         return mm(vv, tile)
 
-    carry = lax.fori_loop(0, N, down_first, jnp.concatenate([zero_v, zero_m, eye], axis=0))
+    carry = run(N, down_first, jnp.concatenate([zero_v, zero_m, eye], axis=0))
     g_c[c, EH:ES] = carry[:R]
     g_c[c, EN:EK] = carry[R : R + W]
     g_c[c, EK:EF] = carry[R + W :]
 
+    half = pl.ds(pl.multiple_of(c * (ES // 2), 8), ES // 2)
+
     def gather_first(g, t, me, size, where, sem):
-        copies = spread(g, me, size, where, sem)
-        finish(copies)
+        if size == 2:
+            finish(spread(g, me, size, where, sem))
+        else:
+            copies, passed = [], []
+            for j in range(1, size):
+                source = (me + size - j) % size
+                copies.append(pltpu.make_async_remote_copy(
+                    src_ref=g.at[me, half], dst_ref=g.at[me, half],
+                    send_sem=sem.at[0, j - 1], recv_sem=sem.at[1, j - 1],
+                    device_id=where(j), device_id_type=MESH,
+                ))
+                passed.append(pltpu.make_async_remote_copy(
+                    src_ref=g.at[source, half], dst_ref=g.at[source, half],
+                    send_sem=sem.at[2, j - 1], recv_sem=sem.at[3, j - 1],
+                    device_id=in_c(1), device_id_type=MESH,
+                ))
+            for j in (1, 3, 2):
+                copies[j - 1].start()
+            for j in (1, 3, 2):
+                copies[j - 1].wait_recv()
+                passed[j - 1].start()
+            for copy in copies:
+                copy.wait_send()
+            finish(passed)
         for e in range(size):
             for m in range(3):
                 t[e, m] = tile_of(g[e, m * W : (m + 1) * W])
@@ -208,11 +240,8 @@
     a, l = enter(inside_c, r_c, a, l)
 
     def settle(v, a, l):
-        def one(i, none):
+        for i in range(N):
             v[i] = v[i] + mm_pair(a, l, tab[i])
-            return none
-
-        lax.fori_loop(0, N, one, 0)
 
     settle(v2, a, l)
 
@@ -250,7 +279,7 @@
         zs[i, :R] = mm(yv, tp[i])
         return mm(yv, tu[i])
 
-    h_c[c, :R] = lax.fori_loop(0, N, up, zero_v)
+    h_c[c, :R] = run(N, up, zero_v)
 
     def down(k, carry):
         i = N - 1 - k
@@ -258,7 +287,7 @@
         v1[i] = vv
         return mm(vv, tl[i])
 
-    h_c[c, R:] = lax.fori_loop(0, N, down, zero_v)
+    h_c[c, R:] = run(N, down, zero_v)
 
     finish(spread(h_c, c, 2, in_c, sem_hc))
     (a, l), inside_c = level(vec_small(h_c), t_c, c, 2)
@@ -286,7 +315,7 @@
         ss[i + 1] = operand([sg[q, t, i] for t in range(2) for q in range(4)])
         return none
 
-    lax.fori_loop(0, N, pack, 0)
+    run(N, pack, 0)
 
     finish(in_flight)
     (a, l), inside_z = level(vec_small(h_z), t_z, z, 4)
@@ -328,7 +357,7 @@
             out_ref[k, i] = -(o[:, :W] + o[:, W:])
         return none
 
-    lax.fori_loop(0, N, grads, 0)
+    run(N, grads, 0)
 
 
 def body(upper_unit, lower_unit, pivot_inv, loss_grad_one, loss_grad_two, state_one, state_two):
@@ -368,7 +397,7 @@
             pltpu.VMEM((2, 4, W, W), F32),
             pltpu.VMEM((2, 4, W, W), F32),
             pltpu.VMEM((N, 2 * R, 2 * W), BF16),
-            dma((2, 1)), dma((2, 3)), dma((2, 3)),
+            dma((2, 1)), dma((4, 3)), dma((4, 3)),
             dma((2, 1)), dma((2, 3)), dma((2, 3)),
             dma((2, 3)), dma((2,)), dma((2, 2, 4)), dma((2, 2, 3)),
         ],

time: 80.5 us -> 62.2 us (0.77)
  Pallas kernels: 77.8 us -> 59.6 us
    pallas_call x1, Pallas kernels: 77.8 us -> 59.6 us  [body(): pl.pallas_call(kernel, out_shape=jax.ShapeDtypeStruct((3, N, R, W), F32),...]
where the time goes in v2:
time: 62.2 us; the launch traced here: 62 us
  Pallas kernels  59.6 us (96%)
  local copies, waits for them, and re-layouts  2.47 us (4%)
    pallas_call x1, Pallas kernels, body(): pl.pallas_call(kernel, out_shape=jax.ShapeDtypeStruct((3, N, R, W), F32),...  59.6 us
    transpose x1, local copies, waits for them, and re-layouts, body(): return jnp.transpose(grads, (2, 0, 1, 3))  2.47 us

profile of v2, /device:TPU:0, one launch (start us, length us, event | category | flops | bytes accessed | tf_op | source)
XLA Modules:
  0.0 62.0 jit_solution(17456849089131208206)
XLA Ops:
  0.0 59.6 %shard_map.73 = f32[3,16,32,128]{3,2,1,0:T(8,128)} custom-call(f32[16,128,128]{2,1,0:T(8,128)} %u_ref.1, f32[16,128,128]{2,1,0:T(8,128)} %l_ref.1, f32[16,128,128]{2,1,0:T(8,128)} %p_ref.1, f32[16,32,128]{2,1,0:T(8,128)} %g1_ref.1, f32[16,32,128]{2,1,0:T(8,128)} %g2_ref.1, f32[16,32,128]{2,1,0:T(8,128)} %s1_ref.1, f32[16,32,128]{2,1,0:T(8,128)} %s2_ref.1), custom_call_target="tpu_custom_call" | custom-call | tf_op jit(solution)/shard_map/pallas_call | solution.py:368
  59.6 2.5 %copy.8 = f32[32,3,16,128]{3,2,1,0:T(8,128)} copy(f32[32,3,16,128]{3,0,2,1:T(8,128)} %bitcast.1) | data formatting | bytes 1572864 | tf_op jit(solution)/shard_map/transpose | solution.py:408

commit v3 on v1

--- a/solution.py
+++ b/solution.py
@@ -10,7 +10,8 @@
 N = 16
 W = 128
 R = 32
-EM, EN, EK, EF, EH, ES = 0, 128, 256, 384, 416, 448
+EM, EK, EF, EN, EH, ES = 0, 128, 256, 288, 416, 448
+PARTS = ((0, EN), (EN, ES - EN))
 
 
 def split(x):
@@ -44,11 +45,12 @@
 
 
 def kernel(
-    u_ref, l_ref, p_ref, g1_ref, g2_ref, s1_ref, s2_ref, out_ref,
+    u_in, l_in, p_in, g1_in, g2_in, s1_ref, s2_ref, out_ref,
+    u_ref, l_ref, p_ref, g1_ref, g2_ref,
     tu, tp, tl, tab, zs, v2, v1,
-    g_c, g_z, g_y, t_c, t_z, t_y, h_c, h_z, h_y, r_c, r_z, ae, le,
+    g_c, g_z, g_y, t_c, t_z, t_y, h_c, h_z, h_y, r_c, r_z, ae_c, ae_z, ke, ae, le,
     sg, halo, ss, ps, pr, lt,
-    sem_c, sem_z, sem_y, sem_hc, sem_hz, sem_hy, sem_s, sem_own, sem_halo, sem_p,
+    sem_c, sem_z, sem_y, sem_hc, sem_hz, sem_hy, sem_s, sem_own, sem_halo, sem_p, sem_in,
 ):
     d = lax.axis_index("rows")
     x = lax.axis_index("rhs")
@@ -72,15 +74,20 @@
     peers = [in_c(1)] + [f(j) for f in (in_z, in_y, in_x) for j in (1, 2, 3)] + [after, before]
     for peer in peers:
         pl.semaphore_signal(barrier, inc=1, device_id=peer, device_id_type=MESH)
-    pl.semaphore_wait(barrier, len(peers))
-
+
+    loads = [
+        pltpu.make_async_copy(src, dst, sem_in.at[k])
+        for k, (src, dst) in enumerate((
+            (u_in, u_ref), (l_in, l_ref), (g2_in, g2_ref), (p_in, p_ref), (g1_in, g1_ref)
+        ))
+    ]
+    for copy in loads:
+        copy.start()
     own = [
         pltpu.make_async_copy(s, sg.at[x, t], sem_own.at[t]) for t, s in enumerate((s1_ref, s2_ref))
     ]
     for copy in own:
         copy.start()
-    for copy in own:
-        copy.wait()
     states = [
         pltpu.make_async_remote_copy(
             src_ref=sg.at[x], dst_ref=sg.at[x],
@@ -89,8 +96,14 @@
         )
         for j in (1, 3, 2)
     ]
-    for copy in states:
-        copy.start()
+
+    def run(steps, step, carry, by=4):
+        def some(b, carry):
+            for s in range(by):
+                carry = step(b * by + s, carry)
+            return carry
+
+        return lax.fori_loop(0, steps // by, some, carry)
 
     def spread(ref, me, size, where, sem):
         copies = [
@@ -115,57 +128,160 @@
     zero_m = jnp.zeros((W, W), F32)
     zero_v = jnp.zeros((R, W), F32)
 
-    def up_first(i, carry):
-        tile = tile_of(u_ref[i])
+    def first(i, carry):
+        right, left = carry
+        tile, tile_p = tile_of(u_ref[i]), tile_of(p_ref[i])
         tu[i] = tile
-        tile_p = tile_of(p_ref[i])
         tp[i] = tile_p
-        yv = jnp.concatenate([g2_ref[i], zero_m], axis=0) - carry
+        yv = jnp.concatenate([g2_ref[i], zero_m], axis=0) - right
         zs[i] = mm(yv, tile_p)
-        return mm(yv, tile)
-
-    carry = lax.fori_loop(0, N, up_first, jnp.concatenate([zero_v, eye], axis=0))
-    g_c[c, EF:EH] = carry[:R]
-    g_c[c, EM:EN] = carry[R:]
-
-    def down_first(k, carry):
+        k = N - 1 - i
+        tile_l = tile_of(l_ref[k])
+        tl[k] = tile_l
+        vv = -left
+        hi, lo = split(vv)
+        tab[k, W:] = jnp.concatenate([hi, lo], axis=1)
+        return mm(yv, tile), mm(vv, tile_l)
+
+    for copy in loads:
+        copy.wait()
+    right, left = run(N, first, (jnp.concatenate([zero_v, eye], axis=0), eye))
+    g_c[c, EF:EN] = right[:R]
+    g_c[c, EM:EK] = right[R:]
+    g_c[c, EK:EF] = left
+
+    pl.semaphore_wait(barrier, len(peers))
+
+    def pair(part):
+        rows = pl.ds(*PARTS[part])
+        copy = pltpu.make_async_remote_copy(
+            src_ref=g_c.at[c, rows], dst_ref=g_c.at[c, rows],
+            send_sem=sem_c.at[part, 0], recv_sem=sem_c.at[part, 1],
+            device_id=in_c(1), device_id_type=MESH,
+        )
+        copy.start()
+        return copy
+
+    def send_part(g, part, me, where, sem):
+        low, size = PARTS[part]
+        rows = pl.ds(pl.multiple_of(low + c * (size // 2), 8), size // 2)
+        copies, passed = [], []
+        for j in range(1, 4):
+            source = (me + 4 - j) % 4
+            copies.append(pltpu.make_async_remote_copy(
+                src_ref=g.at[me, rows], dst_ref=g.at[me, rows],
+                send_sem=sem.at[part, 0, j - 1], recv_sem=sem.at[part, 1, j - 1],
+                device_id=where(j), device_id_type=MESH,
+            ))
+            passed.append(pltpu.make_async_remote_copy(
+                src_ref=g.at[source, rows], dst_ref=g.at[source, rows],
+                send_sem=sem.at[part, 2, j - 1], recv_sem=sem.at[part, 3, j - 1],
+                device_id=in_c(1), device_id_type=MESH,
+            ))
+        for j in (1, 3, 2):
+            copies[j - 1].start()
+        return copies, passed
+
+    def pass_on(flight):
+        copies, passed = flight
+        for j in (1, 3, 2):
+            copies[j - 1].wait_recv()
+            passed[j - 1].start()
+
+    def land(flight):
+        copies, passed = flight
+        for copy in copies:
+            copy.wait_send()
+        for copy in passed:
+            copy.wait()
+
+    def tiles_mk(g, t, size):
+        for e in range(size):
+            t[e, 0] = tile_of(g[e, EM:EK])
+            t[e, 2] = tile_of(g[e, EK:EF])
+
+    def tiles_n(g, t, size):
+        for e in range(size):
+            t[e, 1] = tile_of(g[e, EN:EH])
+
+    def level_mk(g, t, r, kept, me, size):
+        a = jnp.concatenate([zero_v, eye], axis=0)
+        k = eye
+        for e in range(size):
+            kept[e] = a
+            a = mm(a, t[e, 0]) + jnp.concatenate([g[e, EF:EN], zero_m], axis=0)
+            ke[size - 1 - e] = k
+            k = mm(k, t[size - 1 - e, 2])
+        r[0] = tile_of(kept[me, R:])
+        r[2] = tile_of(ke[me])
+        return a, k, kept[me, :R]
+
+    def level_n(g, t, r, kept, me, size):
+        l = jnp.concatenate([zero_v, zero_m], axis=0)
+        for e in reversed(range(size)):
+            le[e] = l
+            l = (
+                mm(l, t[e, 2])
+                + jnp.concatenate([g[e, EH:ES], zero_m], axis=0)
+                + mm(kept[e], t[e, 1])
+            )
+        r[1] = tile_of(le[me, R:])
+        return l, le[me, :R]
+
+    def put_mk(g, me, a, k):
+        g[me, EF:EN] = a[:R]
+        g[me, EM:EK] = a[R:]
+        g[me, EK:EF] = k
+
+    def put_n(g, me, l):
+        g[me, EH:ES] = l[:R]
+        g[me, EN:EH] = l[R:]
+
+    def second(k, carry):
         i = N - 1 - k
-        tile = tile_of(l_ref[i])
-        tl[i] = tile
-        vv = jnp.concatenate([zs[i], zero_m], axis=0) - carry
+        vv = zs[i] - carry
         v2[i] = vv[:R]
         hi, lo = split(vv[R:])
-        tab[i] = jnp.concatenate([hi, lo], axis=1)
-        return mm(vv, tile)
-
-    carry = lax.fori_loop(0, N, down_first, jnp.concatenate([zero_v, zero_m, eye], axis=0))
-    g_c[c, EH:ES] = carry[:R]
-    g_c[c, EN:EK] = carry[R : R + W]
-    g_c[c, EK:EF] = carry[R + W :]
-
-    def gather_first(g, t, me, size, where, sem):
-        copies = spread(g, me, size, where, sem)
-        finish(copies)
-        for e in range(size):
-            for m in range(3):
-                t[e, m] = tile_of(g[e, m * W : (m + 1) * W])
-
-    def level_maps(g, t, r, me, size):
-        a = jnp.concatenate([zero_v, eye], axis=0)
-        many = []
-        for e in range(size):
-            ae[e] = a
-            many.append(a)
-            a = mm(a, t[e, 0]) + jnp.concatenate([g[e, EF:EH], zero_m], axis=0)
-        l = jnp.concatenate([zero_v, zero_m, eye], axis=0)
-        for e in reversed(range(size)):
-            le[e] = l
-            source = jnp.concatenate([g[e, EH:ES], zero_m], axis=0) + mm(many[e], t[e, 1])
-            l = mm(l, t[e, 2]) + jnp.concatenate([source, zero_m], axis=0)
-        r[0] = tile_of(ae[me, R:])
-        r[1] = tile_of(le[me, R : R + W])
-        r[2] = tile_of(le[me, R + W :])
-        return (a, l), (ae[me, :R], le[me, :R])
+        tab[i, :W] = jnp.concatenate([hi, lo], axis=1)
+        return mm(vv, tl[i])
+
+    c1 = pair(0)
+    for copy in own:
+        copy.wait()
+    for copy in states:
+        copy.start()
+    carry = run(N // 2, second, jnp.concatenate([zero_v, zero_m], axis=0))
+    c1.wait()
+    tiles_mk(g_c, t_c, 2)
+    a_tot, k_tot, a_c = level_mk(g_c, t_c, r_c, ae_c, c, 2)
+    put_mk(g_z, z, a_tot, k_tot)
+    z1 = send_part(g_z, 0, z, in_z, sem_z)
+    carry = run(N // 2, lambda k, v: second(k + N // 2, v), carry)
+    put_n(g_c, c, carry)
+    c2 = pair(1)
+    c2.wait()
+    tiles_n(g_c, t_c, 2)
+    l_tot, l_c = level_n(g_c, t_c, r_c, ae_c, c, 2)
+    put_n(g_z, z, l_tot)
+    z2 = send_part(g_z, 1, z, in_z, sem_z)
+    pass_on(z1)
+    land(z1)
+    tiles_mk(g_z, t_z, 4)
+    a_tot, k_tot, a_z = level_mk(g_z, t_z, r_z, ae_z, z, 4)
+    put_mk(g_y, y, a_tot, k_tot)
+    y1 = send_part(g_y, 0, y, in_y, sem_y)
+    pass_on(z2)
+    land(z2)
+    tiles_n(g_z, t_z, 4)
+    l_tot, l_z = level_n(g_z, t_z, r_z, ae_z, z, 4)
+    put_n(g_y, y, l_tot)
+    y2 = send_part(g_y, 1, y, in_y, sem_y)
+    pass_on(y1)
+    land(y1)
+    tiles_mk(g_y, t_y, 4)
+    pass_on(y2)
+    land(y2)
+    tiles_n(g_y, t_y, 4)
 
     def level(vec, t, me, size):
         a = zero_v
@@ -180,39 +296,22 @@
             l = mm(l, t[e, 2]) + (vec(e, 1) + mm(many[e], t[e, 1]))
         return (a, l), (ae[me, :R], le[me, :R])
 
-    def put(g, me, a, l):
-        g[me, EF:EH] = a[:R]
-        g[me, EM:EN] = a[R:]
-        g[me, EH:ES] = l[:R]
-        g[me, EN:EK] = l[R : R + W]
-        g[me, EK:EF] = l[R + W :]
-
     def enter(inside, r, a, l):
         return inside[0] + mm(a, r[0]), inside[1] + mm(a, r[1]) + mm(l, r[2])
 
     def vec_of(g):
-        return lambda e, side: g[e, EF + R * side : EF + R * side + R]
+        return lambda e, side: g[e, EH:ES] if side else g[e, EF:EN]
 
     def vec_small(h):
         return lambda e, side: h[e, R * side : R * side + R]
 
-    gather_first(g_c, t_c, c, 2, in_c, sem_c)
-    total, inside_c = level_maps(g_c, t_c, r_c, c, 2)
-    put(g_z, z, *total)
-    gather_first(g_z, t_z, z, 4, in_z, sem_z)
-    total, inside_z = level_maps(g_z, t_z, r_z, z, 4)
-    put(g_y, y, *total)
-    gather_first(g_y, t_y, y, 4, in_y, sem_y)
     _, (a, l) = level(vec_of(g_y), t_y, y, 4)
-    a, l = enter(inside_z, r_z, a, l)
-    a, l = enter(inside_c, r_c, a, l)
+    a, l = enter((a_z, l_z), r_z, a, l)
+    a, l = enter((a_c, l_c), r_c, a, l)
 
     def settle(v, a, l):
-        def one(i, none):
+        for i in range(N):
             v[i] = v[i] + mm_pair(a, l, tab[i])
-            return none
-
-        lax.fori_loop(0, N, one, 0)
 
     settle(v2, a, l)
 
@@ -250,7 +349,7 @@
         zs[i, :R] = mm(yv, tp[i])
         return mm(yv, tu[i])
 
-    h_c[c, :R] = lax.fori_loop(0, N, up, zero_v)
+    h_c[c, :R] = run(N, up, zero_v)
 
     def down(k, carry):
         i = N - 1 - k
@@ -258,7 +357,7 @@
         v1[i] = vv
         return mm(vv, tl[i])
 
-    h_c[c, R:] = lax.fori_loop(0, N, down, zero_v)
+    h_c[c, R:] = run(N, down, zero_v)
 
     finish(spread(h_c, c, 2, in_c, sem_hc))
     (a, l), inside_c = level(vec_small(h_c), t_c, c, 2)
@@ -286,7 +385,7 @@
         ss[i + 1] = operand([sg[q, t, i] for t in range(2) for q in range(4)])
         return none
 
-    lax.fori_loop(0, N, pack, 0)
+    run(N, pack, 0)
 
     finish(in_flight)
     (a, l), inside_z = level(vec_small(h_z), t_z, z, 4)
@@ -328,7 +427,7 @@
             out_ref[k, i] = -(o[:, :W] + o[:, W:])
         return none
 
-    lax.fori_loop(0, N, grads, 0)
+    run(N, grads, 0)
 
 
 def body(upper_unit, lower_unit, pivot_inv, loss_grad_one, loss_grad_two, state_one, state_two):
@@ -339,9 +438,14 @@
     grads = pl.pallas_call(
         kernel,
         out_shape=jax.ShapeDtypeStruct((3, N, R, W), F32),
-        in_specs=[vmem] * 5 + [anywhere] * 2,
+        in_specs=[anywhere] * 7,
         out_specs=vmem,
         scratch_shapes=[
+            pltpu.VMEM((N, W, W), F32),
+            pltpu.VMEM((N, W, W), F32),
+            pltpu.VMEM((N, W, W), F32),
+            pltpu.VMEM((N, R, W), F32),
+            pltpu.VMEM((N, R, W), F32),
             pltpu.VMEM((N, *tile), BF16),
             pltpu.VMEM((N, *tile), BF16),
             pltpu.VMEM((N, *tile), BF16),
@@ -360,17 +464,20 @@
             pltpu.VMEM((4, 2 * R, W), F32),
             pltpu.VMEM((3, *tile), BF16),
             pltpu.VMEM((3, *tile), BF16),
+            pltpu.VMEM((2, R + W, W), F32),
             pltpu.VMEM((4, R + W, W), F32),
-            pltpu.VMEM((4, R + 2 * W, W), F32),
+            pltpu.VMEM((4, W, W), F32),
+            pltpu.VMEM((4, R, W), F32),
+            pltpu.VMEM((4, R + W, W), F32),
             pltpu.VMEM((4, 2, N, R, W), F32),
             pltpu.VMEM((2, 4, 2, R, W), F32),
             pltpu.VMEM((N + 2, *tile), BF16),
             pltpu.VMEM((2, 4, W, W), F32),
             pltpu.VMEM((2, 4, W, W), F32),
             pltpu.VMEM((N, 2 * R, 2 * W), BF16),
+            dma((2, 2)), dma((2, 4, 3)), dma((2, 4, 3)),
             dma((2, 1)), dma((2, 3)), dma((2, 3)),
-            dma((2, 1)), dma((2, 3)), dma((2, 3)),
-            dma((2, 3)), dma((2,)), dma((2, 2, 4)), dma((2, 2, 3)),
+            dma((2, 3)), dma((2,)), dma((2, 2, 4)), dma((2, 2, 3)), dma((5,)),
         ],
         compiler_params=pltpu.CompilerParams(
             collective_id=0, has_side_effects=True, vmem_limit_bytes=60 * 2**20

time: 80.5 us -> 56.5 us (0.70)
  Pallas kernels: 77.8 us -> 53.8 us
    pallas_call x1, Pallas kernels: 77.8 us -> 53.8 us  [body(): pl.pallas_call(kernel, out_shape=jax.ShapeDtypeStruct((3, N, R, W), F32),...]
where the time goes in v3:
time: 56.5 us; the launch traced here: 56.3 us
  Pallas kernels  53.8 us (95%)
  local copies, waits for them, and re-layouts  2.47 us (4%)
    pallas_call x1, Pallas kernels, body(): pl.pallas_call(kernel, out_shape=jax.ShapeDtypeStruct((3, N, R, W), F32),...  53.8 us
    transpose x1, local copies, waits for them, and re-layouts, body(): return jnp.transpose(grads, (2, 0, 1, 3))  2.47 us

profile of v3, /device:TPU:0, one launch (start us, length us, event | category | flops | bytes accessed | tf_op | source)
XLA Modules:
  0.0 56.3 jit_solution(3551654730121934490)
XLA Ops:
  0.0 53.8 %shard_map.73 = f32[3,16,32,128]{3,2,1,0:T(8,128)} custom-call(f32[16,128,128]{2,1,0:T(8,128)} %u_in.1, f32[16,128,128]{2,1,0:T(8,128)} %l_in.1, f32[16,128,128]{2,1,0:T(8,128)} %p_in.1, f32[16,32,128]{2,1,0:T(8,128)} %g1_in.1, f32[16,32,128]{2,1,0:T(8,128)} %g2_in.1, f32[16,32,128]{2,1,0:T(8,128)} %s1_ref.1, f32[16,32,128]{2,1,0:T(8,128)} %s2_ref.1), custom_call_target="tpu_custom_call" | custom-call | tf_op jit(solution)/shard_map/pallas_call | solution.py:438
  53.8 2.5 %copy.8 = f32[32,3,16,128]{3,2,1,0:T(8,128)} copy(f32[32,3,16,128]{3,0,2,1:T(8,128)} %bitcast.1) | data formatting | bytes 1572864 | tf_op jit(solution)/shard_map/transpose | solution.py:486

commit v4 on v3

--- a/solution.py
+++ b/solution.py
@@ -47,10 +47,10 @@
 def kernel(
     u_in, l_in, p_in, g1_in, g2_in, s1_ref, s2_ref, out_ref,
     u_ref, l_ref, p_ref, g1_ref, g2_ref,
-    tu, tp, tl, tab, zs, v2, v1,
+    tu, tp, tl, tab, tab1, zs, zs3, v2, v1, base, sl, fh, tfh, al,
     g_c, g_z, g_y, t_c, t_z, t_y, h_c, h_z, h_y, r_c, r_z, ae_c, ae_z, ke, ae, le,
     sg, halo, ss, ps, pr, lt,
-    sem_c, sem_z, sem_y, sem_hc, sem_hz, sem_hy, sem_s, sem_own, sem_halo, sem_p, sem_in,
+    sem_c, sem_z, sem_y, sem_hc, sem_hz, sem_hy, sem_s, sem_own, sem_halo, sem_p, sem_in, sem_al,
 ):
     d = lax.axis_index("rows")
     x = lax.axis_index("rhs")
@@ -264,6 +264,28 @@
     l_tot, l_c = level_n(g_c, t_c, r_c, ae_c, c, 2)
     put_n(g_z, z, l_tot)
     z2 = send_part(g_z, 1, z, in_z, sem_z)
+
+    def third(i, carry):
+        responses = tab[i, :, :W].astype(F32) + tab[i, :, W:].astype(F32)
+        yv = jnp.concatenate([g1_ref[i] + v2[i], responses], axis=0) - carry
+        zs3[i] = mm(yv, tp[i])
+        return mm(yv, tu[i])
+
+    def fourth(k, carry):
+        i = N - 1 - k
+        vv = zs3[i] - carry
+        v1[i] = vv[:R]
+        hi, lo = split(vv[R:])
+        tab1[i] = jnp.concatenate([hi, lo], axis=1)
+        return mm(vv, tl[i])
+
+    def keep_ends(side, carry):
+        fh[side] = carry[:R]
+        hi, lo = split(carry[R:])
+        tfh[side] = jnp.concatenate([hi, lo], axis=1)
+
+    nothing = jnp.zeros((R + 2 * W, W), F32)
+    keep_ends(0, run(N, third, nothing))
     pass_on(z1)
     land(z1)
     tiles_mk(g_z, t_z, 4)
@@ -276,6 +298,7 @@
     l_tot, l_z = level_n(g_z, t_z, r_z, ae_z, z, 4)
     put_n(g_y, y, l_tot)
     y2 = send_part(g_y, 1, y, in_y, sem_y)
+    keep_ends(1, run(N, fourth, nothing))
     pass_on(y1)
     land(y1)
     tiles_mk(g_y, t_y, 4)
@@ -283,18 +306,22 @@
     land(y2)
     tiles_n(g_y, t_y, 4)
 
-    def level(vec, t, me, size):
-        a = zero_v
-        many = []
+    def level(vec, t, me, size, top=False):
+        many = [zero_v, vec(0, 0)]
+        for e in range(1, size - 1 if top else size):
+            many.append(mm(many[e], t[e, 0]) + vec(e, 0))
         for e in range(size):
-            ae[e, :R] = a
-            many.append(a)
-            a = mm(a, t[e, 0]) + vec(e, 0)
+            ae[e, :R] = many[e]
         l = zero_v
         for e in reversed(range(size)):
             le[e, :R] = l
-            l = mm(l, t[e, 2]) + (vec(e, 1) + mm(many[e], t[e, 1]))
-        return (a, l), (ae[me, :R], le[me, :R])
+            if top and e == 0:
+                break
+            pushed = vec(e, 1)
+            if e > 0:
+                pushed = pushed + mm(many[e], t[e, 1])
+            l = pushed if e == size - 1 else mm(l, t[e, 2]) + pushed
+        return (many[-1], l), (ae[me, :R], le[me, :R])
 
     def enter(inside, r, a, l):
         return inside[0] + mm(a, r[0]), inside[1] + mm(a, r[1]) + mm(l, r[2])
@@ -305,15 +332,19 @@
     def vec_small(h):
         return lambda e, side: h[e, R * side : R * side + R]
 
-    _, (a, l) = level(vec_of(g_y), t_y, y, 4)
+    _, (a, l) = level(vec_of(g_y), t_y, y, 4, True)
     a, l = enter((a_z, l_z), r_z, a, l)
     a, l = enter((a_c, l_c), r_c, a, l)
 
-    def settle(v, a, l):
+    def settle(v, tiles, a, l):
         for i in range(N):
-            v[i] = v[i] + mm_pair(a, l, tab[i])
-
-    settle(v2, a, l)
+            v[i] = v[i] + mm_pair(a, l, tiles[i])
+
+    h_c[c, :R] = fh[0] + mm_pair(a, l, tfh[0])
+    h_c[c, R:] = fh[1] + mm_pair(a, l, tfh[1])
+    in_flight = spread(h_c, c, 2, in_c, sem_hc)
+    settle(v2, tab, a, l)
+    settle(v1, tab1, a, l)
 
     block_of = lax.broadcasted_iota(jnp.int32, (W, W), 1) // R
 
@@ -325,9 +356,6 @@
                 if q != dest:
                     moved = pltpu.roll(groups[q], (R * (q - dest)) % W, 1)
                     piece = jnp.where(block_of == q, moved, piece)
-            if True:
-                own_q = groups[dest]
-                piece = jnp.where(block_of == dest, own_q, piece)
             ps[t, dest] = piece
         pr[t, x] = ps[t, x]
         copies = [
@@ -342,28 +370,13 @@
             copy.start()
         return copies
 
-    shared_two = share(v2, 1)
-
-    def up(i, carry):
-        yv = g1_ref[i] + v2[i] - carry
-        zs[i, :R] = mm(yv, tp[i])
-        return mm(yv, tu[i])
-
-    h_c[c, :R] = run(N, up, zero_v)
-
-    def down(k, carry):
-        i = N - 1 - k
-        vv = zs[i, :R] - carry
-        v1[i] = vv
-        return mm(vv, tl[i])
-
-    h_c[c, R:] = run(N, down, zero_v)
-
-    finish(spread(h_c, c, 2, in_c, sem_hc))
+    finish(in_flight)
     (a, l), inside_c = level(vec_small(h_c), t_c, c, 2)
     h_z[z, :R] = a
     h_z[z, R:] = l
     in_flight = spread(h_z, z, 4, in_z, sem_hz)
+    shared_two = share(v2, 1)
+    shared_one = share(v1, 0)
 
     finish(states)
     edges = []
@@ -393,32 +406,58 @@
     h_y[y, R:] = l
     in_flight = spread(h_y, y, 4, in_y, sem_hy)
 
+    row = lax.broadcasted_iota(jnp.int32, (2 * R, 2 * W), 0)
+    lane = lax.broadcasted_iota(jnp.int32, (2 * R, 2 * W), 1)
+    pick = (lane == R * x + row + jnp.where(row < R, 0, W - R)).astype(F32).astype(BF16)
+    by_lanes = (((1,), (1,)), ((), ()))
+    for i in range(N):
+        sl[i] = lax.dot_general(pick, tab[i], by_lanes, preferred_element_type=F32).astype(BF16)
+
     finish(edges)
     keep = ((d > 0).astype(F32), (d < 31).astype(F32))
     for side, slot in ((0, 0), (1, N + 1)):
         ss[slot] = operand([halo[side, q, t] * keep[side] for t in range(2) for q in range(4)])
 
     finish(in_flight)
-    _, (a, l) = level(vec_small(h_y), t_y, y, 4)
+    _, (a, l) = level(vec_small(h_y), t_y, y, 4, True)
     a, l = enter(inside_z, r_z, a, l)
     a, l = enter(inside_c, r_c, a, l)
-    settle(v1, a, l)
-    finish(shared_two)
-    shared_one = share(v1, 0)
+    al[x, :, :W] = a
+    al[x, :, W:] = l
+    in_flight = spread(al, x, 4, in_x, sem_al)
 
     def turn(t):
         for sub in range(4):
             stack = jnp.concatenate(
                 [pr[t, q, R * sub : R * sub + R] for q in range(4)], axis=0
             ).T
+            if t == 0:
+                for q in range(4):
+                    base[4 * q + sub] = stack[R * q : R * q + R]
+                continue
             hi, lo = split(stack)
             for q in range(4):
                 lt[4 * q + sub, :R, t * W : (t + 1) * W] = hi[R * q : R * q + R]
                 lt[4 * q + sub, R:, t * W : (t + 1) * W] = lo[R * q : R * q + R]
 
+    finish(shared_two)
     turn(1)
     finish(shared_one)
     turn(0)
+    finish(in_flight)
+    hi, lo = split(jnp.concatenate([al[q] for q in range(4)], axis=0))
+    arrived = jnp.concatenate([hi, lo], axis=0)
+    for q in range(4):
+        o = lax.dot_general(
+            sl[4 * q : 4 * q + 4].reshape(2 * W, 2 * W), arrived, by_lanes,
+            preferred_element_type=F32,
+        )
+        o = o[:, :W] + o[:, W:]
+        for sub in range(4):
+            i, low = 4 * q + sub, 2 * R * sub
+            hi, lo = split(base[i] + o[low : low + R] + o[low + R : low + 2 * R])
+            lt[i, :R, :W] = hi
+            lt[i, R:, :W] = lo
 
     def grads(i, none):
         for k, j in enumerate((1, 0, 2)):
@@ -450,9 +489,16 @@
             pltpu.VMEM((N, *tile), BF16),
             pltpu.VMEM((N, *tile), BF16),
             pltpu.VMEM((N, *tile), BF16),
+            pltpu.VMEM((N, *tile), BF16),
             pltpu.VMEM((N, R + W, W), F32),
+            pltpu.VMEM((N, R + 2 * W, W), F32),
             pltpu.VMEM((N, R, W), F32),
             pltpu.VMEM((N, R, W), F32),
+            pltpu.VMEM((N, R, W), F32),
+            pltpu.VMEM((N, 2 * R, 2 * W), BF16),
+            pltpu.VMEM((2, R, W), F32),
+            pltpu.VMEM((2, *tile), BF16),
+            pltpu.VMEM((4, R, 2 * W), F32),
             pltpu.VMEM((2, ES, W), F32),
             pltpu.VMEM((4, ES, W), F32),
             pltpu.VMEM((4, ES, W), F32),
@@ -477,7 +523,7 @@
             pltpu.VMEM((N, 2 * R, 2 * W), BF16),
             dma((2, 2)), dma((2, 4, 3)), dma((2, 4, 3)),
             dma((2, 1)), dma((2, 3)), dma((2, 3)),
-            dma((2, 3)), dma((2,)), dma((2, 2, 4)), dma((2, 2, 3)), dma((5,)),
+            dma((2, 3)), dma((2,)), dma((2, 2, 4)), dma((2, 2, 3)), dma((5,)), dma((2, 3)),
         ],
         compiler_params=pltpu.CompilerParams(
             collective_id=0, has_side_effects=True, vmem_limit_bytes=60 * 2**20

time: 56.5 us -> 49.4 us (0.87)
  Pallas kernels: 53.8 us -> 46.8 us
    pallas_call x1, Pallas kernels: 53.8 us -> 46.8 us  [body(): pl.pallas_call(kernel, out_shape=jax.ShapeDtypeStruct((3, N, R, W), F32),...]
where the time goes in v4:
time: 49.4 us; the launch traced here: 49.2 us
  Pallas kernels  46.8 us (95%)
  local copies, waits for them, and re-layouts  2.47 us (5%)
    pallas_call x1, Pallas kernels, body(): pl.pallas_call(kernel, out_shape=jax.ShapeDtypeStruct((3, N, R, W), F32),...  46.8 us
    transpose x1, local copies, waits for them, and re-layouts, body(): return jnp.transpose(grads, (2, 0, 1, 3))  2.47 us

profile of v4, /device:TPU:0, one launch (start us, length us, event | category | flops | bytes accessed | tf_op | source)
XLA Modules:
  0.0 49.2 jit_solution(13555764891766501561)
XLA Ops:
  0.0 46.8 %shard_map.73 = f32[3,16,32,128]{3,2,1,0:T(8,128)} custom-call(f32[16,128,128]{2,1,0:T(8,128)} %u_in.1, f32[16,128,128]{2,1,0:T(8,128)} %l_in.1, f32[16,128,128]{2,1,0:T(8,128)} %p_in.1, f32[16,32,128]{2,1,0:T(8,128)} %g1_in.1, f32[16,32,128]{2,1,0:T(8,128)} %g2_in.1, f32[16,32,128]{2,1,0:T(8,128)} %s1_ref.1, f32[16,32,128]{2,1,0:T(8,128)} %s2_ref.1), custom_call_target="tpu_custom_call" | custom-call | tf_op jit(solution)/shard_map/pallas_call | solution.py:477
  46.8 2.5 %copy.8 = f32[32,3,16,128]{3,2,1,0:T(8,128)} copy(f32[32,3,16,128]{3,0,2,1:T(8,128)} %bitcast.1) | data formatting | bytes 1572864 | tf_op jit(solution)/shard_map/transpose | solution.py:532

commit v5 on v4

--- a/solution.py
+++ b/solution.py
@@ -204,29 +204,39 @@
         for e in range(size):
             t[e, 1] = tile_of(g[e, EN:EH])
 
-    def level_mk(g, t, r, kept, me, size):
-        a = jnp.concatenate([zero_v, eye], axis=0)
-        k = eye
-        for e in range(size):
+    def level_mk(g, t, kept, size):
+        kept[0] = jnp.concatenate([zero_v, eye], axis=0)
+        ke[size - 1] = eye
+        a = jnp.concatenate([g[0, EF:EN], g[0, EM:EK]], axis=0)
+        k = g[size - 1, EK:EF]
+        for e in range(1, size):
             kept[e] = a
             a = mm(a, t[e, 0]) + jnp.concatenate([g[e, EF:EN], zero_m], axis=0)
             ke[size - 1 - e] = k
             k = mm(k, t[size - 1 - e, 2])
+        return a, k
+
+    def own_mk(r, kept, me):
         r[0] = tile_of(kept[me, R:])
         r[2] = tile_of(ke[me])
-        return a, k, kept[me, :R]
-
-    def level_n(g, t, r, kept, me, size):
-        l = jnp.concatenate([zero_v, zero_m], axis=0)
+        return kept[me, :R]
+
+    def level_n(g, t, kept, size):
+        le[size - 1] = jnp.concatenate([zero_v, zero_m], axis=0)
         for e in reversed(range(size)):
-            le[e] = l
-            l = (
-                mm(l, t[e, 2])
-                + jnp.concatenate([g[e, EH:ES], zero_m], axis=0)
-                + mm(kept[e], t[e, 1])
-            )
+            source = jnp.concatenate([g[e, EH:ES], zero_m], axis=0)
+            if e == 0:
+                pushed = source + jnp.concatenate([zero_v, g[0, EN:EH]], axis=0)
+            else:
+                pushed = source + mm(kept[e], t[e, 1])
+            l = pushed if e == size - 1 else mm(l, t[e, 2]) + pushed
+            if e > 0:
+                le[e - 1] = l
+        return l
+
+    def own_n(r, me):
         r[1] = tile_of(le[me, R:])
-        return l, le[me, :R]
+        return le[me, :R]
 
     def put_mk(g, me, a, k):
         g[me, EF:EN] = a[:R]
@@ -253,17 +263,19 @@
     carry = run(N // 2, second, jnp.concatenate([zero_v, zero_m], axis=0))
     c1.wait()
     tiles_mk(g_c, t_c, 2)
-    a_tot, k_tot, a_c = level_mk(g_c, t_c, r_c, ae_c, c, 2)
+    a_tot, k_tot = level_mk(g_c, t_c, ae_c, 2)
     put_mk(g_z, z, a_tot, k_tot)
     z1 = send_part(g_z, 0, z, in_z, sem_z)
+    a_c = own_mk(r_c, ae_c, c)
     carry = run(N // 2, lambda k, v: second(k + N // 2, v), carry)
     put_n(g_c, c, carry)
     c2 = pair(1)
     c2.wait()
     tiles_n(g_c, t_c, 2)
-    l_tot, l_c = level_n(g_c, t_c, r_c, ae_c, c, 2)
+    l_tot = level_n(g_c, t_c, ae_c, 2)
     put_n(g_z, z, l_tot)
     z2 = send_part(g_z, 1, z, in_z, sem_z)
+    l_c = own_n(r_c, c)
 
     def third(i, carry):
         responses = tab[i, :, :W].astype(F32) + tab[i, :, W:].astype(F32)
@@ -289,16 +301,26 @@
     pass_on(z1)
     land(z1)
     tiles_mk(g_z, t_z, 4)
-    a_tot, k_tot, a_z = level_mk(g_z, t_z, r_z, ae_z, z, 4)
+    a_tot, k_tot = level_mk(g_z, t_z, ae_z, 4)
     put_mk(g_y, y, a_tot, k_tot)
     y1 = send_part(g_y, 0, y, in_y, sem_y)
+    a_z = own_mk(r_z, ae_z, z)
     pass_on(z2)
     land(z2)
     tiles_n(g_z, t_z, 4)
-    l_tot, l_z = level_n(g_z, t_z, r_z, ae_z, z, 4)
+    l_tot = level_n(g_z, t_z, ae_z, 4)
     put_n(g_y, y, l_tot)
     y2 = send_part(g_y, 1, y, in_y, sem_y)
+    l_z = own_n(r_z, z)
     keep_ends(1, run(N, fourth, nothing))
+
+    row = lax.broadcasted_iota(jnp.int32, (2 * R, 2 * W), 0)
+    lane = lax.broadcasted_iota(jnp.int32, (2 * R, 2 * W), 1)
+    pick = (lane == R * x + row + jnp.where(row < R, 0, W - R)).astype(F32).astype(BF16)
+    by_lanes = (((1,), (1,)), ((), ()))
+    for i in range(N):
+        sl[i] = lax.dot_general(pick, tab[i], by_lanes, preferred_element_type=F32).astype(BF16)
+
     pass_on(y1)
     land(y1)
     tiles_mk(g_y, t_y, 4)
@@ -378,6 +400,12 @@
     shared_two = share(v2, 1)
     shared_one = share(v1, 0)
 
+    finish(in_flight)
+    (a, l), inside_z = level(vec_small(h_z), t_z, z, 4)
+    h_y[y, :R] = a
+    h_y[y, R:] = l
+    in_flight = spread(h_y, y, 4, in_y, sem_hy)
+
     finish(states)
     edges = []
     for side, (row, where) in enumerate(((N - 1, after), (0, before))):
@@ -399,24 +427,6 @@
         return none
 
     run(N, pack, 0)
-
-    finish(in_flight)
-    (a, l), inside_z = level(vec_small(h_z), t_z, z, 4)
-    h_y[y, :R] = a
-    h_y[y, R:] = l
-    in_flight = spread(h_y, y, 4, in_y, sem_hy)
-
-    row = lax.broadcasted_iota(jnp.int32, (2 * R, 2 * W), 0)
-    lane = lax.broadcasted_iota(jnp.int32, (2 * R, 2 * W), 1)
-    pick = (lane == R * x + row + jnp.where(row < R, 0, W - R)).astype(F32).astype(BF16)
-    by_lanes = (((1,), (1,)), ((), ()))
-    for i in range(N):
-        sl[i] = lax.dot_general(pick, tab[i], by_lanes, preferred_element_type=F32).astype(BF16)
-
-    finish(edges)
-    keep = ((d > 0).astype(F32), (d < 31).astype(F32))
-    for side, slot in ((0, 0), (1, N + 1)):
-        ss[slot] = operand([halo[side, q, t] * keep[side] for t in range(2) for q in range(4)])
 
     finish(in_flight)
     _, (a, l) = level(vec_small(h_y), t_y, y, 4, True)
@@ -444,6 +454,10 @@
     turn(1)
     finish(shared_one)
     turn(0)
+    finish(edges)
+    keep = ((d > 0).astype(F32), (d < 31).astype(F32))
+    for side, slot in ((0, 0), (1, N + 1)):
+        ss[slot] = operand([halo[side, q, t] * keep[side] for t in range(2) for q in range(4)])
     finish(in_flight)
     hi, lo = split(jnp.concatenate([al[q] for q in range(4)], axis=0))
     arrived = jnp.concatenate([hi, lo], axis=0)
@@ -459,24 +473,25 @@
             lt[i, :R, :W] = hi
             lt[i, R:, :W] = lo
 
-    def grads(i, none):
-        for k, j in enumerate((1, 0, 2)):
-            o = jnp.dot(lt[i], ss[i + j], preferred_element_type=F32)
-            o = o[:R] + o[R:]
-            out_ref[k, i] = -(o[:, :W] + o[:, W:])
-        return none
-
-    run(N, grads, 0)
+    for j in range(N + 2):
+        low, high = max(j - 2, 0), min(j + 1, N)
+        o = jnp.dot(
+            lt[low:high].reshape(2 * R * (high - low), 2 * W), ss[j], preferred_element_type=F32
+        )
+        o = o[:, :W] + o[:, W:]
+        for i in range(low, high):
+            at = 2 * R * (i - low)
+            out_ref[(1, 0, 2)[j - i], i] = -(o[at : at + R] + o[at + R : at + 2 * R])
 
 
 def body(upper_unit, lower_unit, pivot_inv, loss_grad_one, loss_grad_two, state_one, state_two):
     vmem = pl.BlockSpec(memory_space=pltpu.VMEM)
-    anywhere = pl.BlockSpec(memory_space=pl.ANY)
+    anywhere = pl.BlockSpec(memory_space=pltpu.HBM)
     dma = pltpu.SemaphoreType.DMA
     tile = (2 * W, 2 * W)
     grads = pl.pallas_call(
         kernel,
-        out_shape=jax.ShapeDtypeStruct((3, N, R, W), F32),
+        out_shape=pltpu.VMEM((3, N, R, W), F32),
         in_specs=[anywhere] * 7,
         out_specs=vmem,
         scratch_shapes=[
@@ -526,7 +541,7 @@
             dma((2, 3)), dma((2,)), dma((2, 2, 4)), dma((2, 2, 3)), dma((5,)), dma((2, 3)),
         ],
         compiler_params=pltpu.CompilerParams(
-            collective_id=0, has_side_effects=True, vmem_limit_bytes=60 * 2**20
+            collective_id=0, has_side_effects=True, vmem_limit_bytes=66_200_000
         ),
     )(upper_unit, lower_unit, pivot_inv, loss_grad_one, loss_grad_two, state_one, state_two)
     return jnp.transpose(grads, (2, 0, 1, 3))

time: 49.4 us -> 45.4 us (0.919)
  Pallas kernels: 46.8 us -> 44 us
  local copies, waits for them, and re-layouts: 2.47 us -> 1.34 us
    pallas_call x1, Pallas kernels: 46.8 us -> 44 us  [body(): pl.pallas_call(kernel, out_shape=pltpu.VMEM((3, N, R, W), F32), in_specs=...]
    transpose x1, local copies, waits for them, and re-layouts: 2.47 us -> 1.34 us  [body(): return jnp.transpose(grads, (2, 0, 1, 3))]
where the time goes in v5:
time: 45.4 us; the launch traced here: 45.3 us
  Pallas kernels  44 us (97%)
  local copies, waits for them, and re-layouts  1.34 us (3%)
    pallas_call x1, Pallas kernels, body(): pl.pallas_call(kernel, out_shape=pltpu.VMEM((3, N, R, W), F32), in_specs=...  44 us
    transpose x1, local copies, waits for them, and re-layouts, body(): return jnp.transpose(grads, (2, 0, 1, 3))  1.34 us

profile of v5, /device:TPU:0, one launch (start us, length us, event | category | flops | bytes accessed | tf_op | source)
XLA Modules:
  0.0 45.3 jit_solution(12355450221225705050)
XLA Ops:
  0.0 44.0 %shard_map.73 = f32[3,16,32,128]{3,2,1,0:T(8,128)S(1)} custom-call(f32[16,128,128]{2,1,0:T(8,128)} %u_in.1, f32[16,128,128]{2,1,0:T(8,128)} %l_in.1, f32[16,128,128]{2,1,0:T(8,128)} %p_in.1, f32[16,32,128]{2,1,0:T(8,128)} %g1_in.1, f32[16,32,128]{2,1,0:T(8,128)} %g2_in.1, f32[16,32,128]{2,1,0:T(8,128)} %s1_ref.1, f32[16,32,128]{2,1,0:T(8,128)} %s2_ref.1), custom_call_target="tpu_custom_call" | custom-call | tf_op jit(solution)/shard_map/pallas_call | solution.py:492
  44.0 1.3 %copy.8 = f32[32,3,16,128]{3,2,1,0:T(8,128)} copy(f32[32,3,16,128]{3,0,2,1:T(8,128)S(1)} %bitcast.1) | data formatting | bytes 1572864 | tf_op jit(solution)/shard_map/transpose | solution.py:547

commit v6 on v5

--- a/solution.py
+++ b/solution.py
@@ -118,9 +118,12 @@
             copy.start()
         return copies
 
+    sent = []
+
     def finish(copies):
         for copy in copies:
-            copy.wait()
+            copy.wait_recv()
+        sent.extend(copies)
 
     eye = (
         lax.broadcasted_iota(jnp.int32, (W, W), 0) == lax.broadcasted_iota(jnp.int32, (W, W), 1)
@@ -190,10 +193,9 @@
 
     def land(flight):
         copies, passed = flight
-        for copy in copies:
-            copy.wait_send()
         for copy in passed:
-            copy.wait()
+            copy.wait_recv()
+        sent.extend(copies + passed)
 
     def tiles_mk(g, t, size):
         for e in range(size):
@@ -261,7 +263,7 @@
     for copy in states:
         copy.start()
     carry = run(N // 2, second, jnp.concatenate([zero_v, zero_m], axis=0))
-    c1.wait()
+    finish([c1])
     tiles_mk(g_c, t_c, 2)
     a_tot, k_tot = level_mk(g_c, t_c, ae_c, 2)
     put_mk(g_z, z, a_tot, k_tot)
@@ -270,7 +272,7 @@
     carry = run(N // 2, lambda k, v: second(k + N // 2, v), carry)
     put_n(g_c, c, carry)
     c2 = pair(1)
-    c2.wait()
+    finish([c2])
     tiles_n(g_c, t_c, 2)
     l_tot = level_n(g_c, t_c, ae_c, 2)
     put_n(g_z, z, l_tot)
@@ -482,6 +484,9 @@
         for i in range(low, high):
             at = 2 * R * (i - low)
             out_ref[(1, 0, 2)[j - i], i] = -(o[at : at + R] + o[at + R : at + 2 * R])
+
+    for copy in sent:
+        copy.wait_send()
 
 
 def body(upper_unit, lower_unit, pivot_inv, loss_grad_one, loss_grad_two, state_one, state_two):

time: 45.4 us -> 45.2 us (level)
  no operation moved by 1% of the time
where the time goes in v6:
time: 45.2 us; the launch traced here: 45.1 us
  Pallas kernels  43.7 us (97%)
  local copies, waits for them, and re-layouts  1.34 us (3%)
    pallas_call x1, Pallas kernels, body(): pl.pallas_call(kernel, out_shape=pltpu.VMEM((3, N, R, W), F32), in_specs=...  43.7 us
    transpose x1, local copies, waits for them, and re-layouts, body(): return jnp.transpose(grads, (2, 0, 1, 3))  1.34 us

profile of v6, /device:TPU:0, one launch (start us, length us, event | category | flops | bytes accessed | tf_op | source)
XLA Modules:
  0.0 45.1 jit_solution(16414608046667003342)
XLA Ops:
  0.0 43.7 %shard_map.73 = f32[3,16,32,128]{3,2,1,0:T(8,128)S(1)} custom-call(f32[16,128,128]{2,1,0:T(8,128)} %u_in.1, f32[16,128,128]{2,1,0:T(8,128)} %l_in.1, f32[16,128,128]{2,1,0:T(8,128)} %p_in.1, f32[16,32,128]{2,1,0:T(8,128)} %g1_in.1, f32[16,32,128]{2,1,0:T(8,128)} %g2_in.1, f32[16,32,128]{2,1,0:T(8,128)} %s1_ref.1, f32[16,32,128]{2,1,0:T(8,128)} %s2_ref.1), custom_call_target="tpu_custom_call" | custom-call | tf_op jit(solution)/shard_map/pallas_call | solution.py:497
  43.8 1.3 %copy.8 = f32[32,3,16,128]{3,2,1,0:T(8,128)} copy(f32[32,3,16,128]{3,0,2,1:T(8,128)S(1)} %bitcast.1) | data formatting | bytes 1572864 | tf_op jit(solution)/shard_map/transpose | solution.py:552
